TPU v7x, 32 devices: a whole 2x2x4 slice. The times are simulated.
32 devices in a mesh: fsdp: 4 (over z), ep: 8 (over y, x, core).
Axes of the slice: x: 2, y: 2, z: 4, core: 2. Of those that a mesh axis runs over, the one named last changes fastest.
Arguments:
- x_tok: bfloat16 [8192, 512], P(('fsdp', 'ep'))
- dy_tok: bfloat16 [8192, 512], P(('fsdp', 'ep'))
- expert_ids: int32 [8192, 2], P(('fsdp', 'ep'))
- route_w: float32 [8192, 2], P(('fsdp', 'ep'))
- w_gate: bfloat16 [8, 512, 1792], P('ep', 'fsdp')
- w_up: bfloat16 [8, 512, 1792], P('ep', 'fsdp')
- w_down: bfloat16 [8, 1792, 512], P('ep', None, 'fsdp')
Outputs:
- output 1: bfloat16 [8192, 512], P(('fsdp', 'ep'))
- output 2: float32 [8192, 2], P(('fsdp', 'ep'))
- output 3: float32 [8, 512, 1792], P('ep', 'fsdp')
- output 4: float32 [8, 512, 1792], P('ep', 'fsdp')
- output 5: float32 [8, 1792, 512], P('ep', None, 'fsdp')
All inputs are finite; a program needn't handle non-finite values.
Results may differ from a plain program's by a relative error of at most 0.00103.
Values are sent between devices in bfloat16 or wider.
A program may use at most 1 GiB of HBM per device.

v0:
```python
import jax
import jax.numpy as jnp
from jax import lax
from jax.sharding import PartitionSpec as P

CAP_FACTOR = 3


def capacity_of(tok_dev, top_k, experts):
    return max(8, ((CAP_FACTOR * tok_dev * top_k // experts + 7) // 8) * 8)


def route_slots(ids_dev, experts, capacity):
    n_pairs = ids_dev.shape[0]
    n_slots = experts * capacity
    onehot = (ids_dev[:, None] == jnp.arange(experts, dtype=jnp.int32)[None, :]).astype(jnp.int32)
    before = jnp.cumsum(onehot, axis=0) - onehot
    position = jnp.sum(before * onehot, axis=1)
    dest_slot = jnp.where(position < capacity, ids_dev * capacity + position, n_slots)
    held = jax.ops.segment_sum(jnp.arange(1, n_pairs + 1, dtype=jnp.int32), dest_slot, num_segments=n_slots + 1)[:n_slots]
    slot_src = jnp.where(held > 0, held - 1, n_pairs)
    return dest_slot, slot_src


def swiglu_grads(pre_gate, pre_up, grad_hidden):
    sigma = jax.nn.sigmoid(pre_gate)
    grad_gate = grad_hidden * pre_up * sigma * (1.0 + pre_gate * (1.0 - sigma))
    grad_up = grad_hidden * pre_gate * sigma
    return grad_gate.astype(jnp.bfloat16), grad_up.astype(jnp.bfloat16)


def expert_backward(x_rows, dy_rows, gate_rows, w_gate_full, w_up_full, w_down_full):
    pre_gate = jnp.einsum("secd,edf->secf", x_rows, w_gate_full, preferred_element_type=jnp.float32)
    pre_up = jnp.einsum("secd,edf->secf", x_rows, w_up_full, preferred_element_type=jnp.float32)
    hidden = (jax.nn.silu(pre_gate) * pre_up).astype(jnp.bfloat16)
    y_rows = jnp.einsum("secf,efd->secd", hidden, w_down_full, preferred_element_type=jnp.float32)
    dy_wide = dy_rows.astype(jnp.float32)
    scaled_dy = (gate_rows[..., None] * dy_wide).astype(jnp.bfloat16)
    dr_rows = jnp.sum(dy_wide * y_rows, axis=-1)
    grad_hidden = jnp.einsum("secd,efd->secf", scaled_dy, w_down_full, preferred_element_type=jnp.float32)
    grad_gate, grad_up = swiglu_grads(pre_gate, pre_up, grad_hidden)
    dx_rows = (jnp.einsum("secf,edf->secd", grad_gate, w_gate_full, preferred_element_type=jnp.float32)
               + jnp.einsum("secf,edf->secd", grad_up, w_up_full, preferred_element_type=jnp.float32)).astype(jnp.bfloat16)
    dw_gate = jnp.einsum("secd,secf->edf", x_rows, grad_gate, preferred_element_type=jnp.float32)
    dw_up = jnp.einsum("secd,secf->edf", x_rows, grad_up, preferred_element_type=jnp.float32)
    dw_down = jnp.einsum("secf,secd->efd", hidden, scaled_dy, preferred_element_type=jnp.float32)
    return dx_rows, dr_rows, dw_gate, dw_up, dw_down


def take_rows(rows, row_ids):
    return jnp.take(rows, row_ids, axis=0, mode="fill", fill_value=0)


def solution(mesh):
    n_ep = mesh.shape["ep"]
    tok_spec = P(("fsdp", "ep"), None)
    spec_in = P("ep", "fsdp", None)
    spec_out = P("ep", None, "fsdp")

    def per_device(x_tok, dy_tok, expert_ids, route_w, w_gate, w_up, w_down):
        tok_dev, top_k = expert_ids.shape
        exp_local = w_gate.shape[0]
        d_model = x_tok.shape[1]
        experts = exp_local * n_ep
        capacity = capacity_of(tok_dev, top_k, experts)
        dest_slot, slot_src = route_slots(expert_ids.reshape(-1), experts, capacity)
        tok_of_slot = slot_src // top_k
        x_send = take_rows(x_tok, tok_of_slot)
        dy_send = take_rows(dy_tok, tok_of_slot)
        gate_send = take_rows(route_w.reshape(-1), slot_src)
        x_recv = lax.all_to_all(x_send, "ep", 0, 0, tiled=True).reshape(n_ep, exp_local, capacity, d_model)
        dy_recv = lax.all_to_all(dy_send, "ep", 0, 0, tiled=True).reshape(n_ep, exp_local, capacity, d_model)
        gate_recv = lax.all_to_all(gate_send, "ep", 0, 0, tiled=True).reshape(n_ep, exp_local, capacity)
        w_gate_full = lax.all_gather(w_gate, "fsdp", axis=1, tiled=True)
        w_up_full = lax.all_gather(w_up, "fsdp", axis=1, tiled=True)
        w_down_full = lax.all_gather(w_down, "fsdp", axis=2, tiled=True)
        dx_rows, dr_rows, dw_gate, dw_up, dw_down = expert_backward(
            x_recv, dy_recv, gate_recv, w_gate_full, w_up_full, w_down_full)
        dx_back = lax.all_to_all(dx_rows.reshape(n_ep * exp_local * capacity, d_model), "ep", 0, 0, tiled=True)
        dr_back = lax.all_to_all(dr_rows.reshape(-1), "ep", 0, 0, tiled=True)
        dx_pairs = take_rows(dx_back, dest_slot).reshape(tok_dev, top_k, d_model)
        grad_x = jnp.sum(dx_pairs.astype(jnp.float32), axis=1).astype(jnp.bfloat16)
        route_grad = take_rows(dr_back, dest_slot).reshape(tok_dev, top_k)
        grad_w_gate = lax.psum_scatter(dw_gate, "fsdp", scatter_dimension=1, tiled=True)
        grad_w_up = lax.psum_scatter(dw_up, "fsdp", scatter_dimension=1, tiled=True)
        grad_w_down = lax.psum_scatter(dw_down, "fsdp", scatter_dimension=2, tiled=True)
        return grad_x, route_grad, grad_w_gate, grad_w_up, grad_w_down

    return jax.shard_map(
        per_device, mesh=mesh,
        in_specs=(tok_spec, tok_spec, tok_spec, tok_spec, spec_in, spec_in, spec_out),
        out_specs=(tok_spec, tok_spec, spec_in, spec_in, spec_out),
        check_vma=False)
```

profile of v0, /device:TPU:0, one launch (start us, length us, event | category | flops | bytes accessed | tf_op | source)
XLA Modules:
  0.0 381.2 jit_solution(4300315044562577525)
XLA Ops:
  7.2 0.0 copy-start
  7.2 0.0 all-gather.8.cloned.1.call-start
  7.2 0.7 all-gather.8.cloned.1.call-update
  7.9 0.0 all-gather.4.cloned.1.call-start
  8.0 0.7 all-gather.4.cloned.1.call-update
  8.7 0.8 copy.18
  9.5 0.1 eq.29
  9.6 0.1 eq.25
  9.8 1.1 reduce-window.6
  10.9 0.2 slice_reduce_fusion
  11.2 0.1 mul.70
  11.3 0.8 copy.21
  12.2 0.1 reshape.234
  12.3 0.1 fusion.53
  12.4 3.5 scatter_custom_fusion
  16.0 9.5 %gather_fusion = f32[1536]{0:T(1024)S(1)} fusion(f32[512]{0:T(512)S(1)} %reshape.234, s32[2048]{0:T(1024)S(1)} %pad_clamp_fusion.1), kind=kCustom, calls=%fused_computation.2 | custom fusion | bytes 18432 | tf_op jit(solution)/shard_map/jit(_take)/gather | solution.py:51
  25.4 0.1 gather.22
  25.5 0.1 select_n.102
  25.6 0.6 and_select_fusion
  26.2 5.3 %all-to-all-start = ((f32[8,192,1]{1,2,0:T(1,128)}), f32[8,192,1]{1,2,0:T(1,128)S(1)}, u32[]{:S(2)}, u32[]{:S(2)}) async-start(f32[8,192,1]{1,2,0:T(1,128)} %and_select_fusion), calls=%async_computation | async-start | bytes 16384 | tf_op jit(solution)/shard_map/all_to_all | solution.py:73
  31.6 0.0 copy-start.2
  31.6 4.8 %gather_fusion.3 = bf16[1536,512]{1,0:T(8,128)(2,1)S(1)} fusion(bf16[256,512]{1,0:T(8,128)(2,1)S(1)} %copy-done, s32[2048]{0:T(1024)S(1)} %pad_clamp_fusion), kind=kCustom, calls=%fused_computation.clone | custom fusion | bytes 3151872 | tf_op jit(solution)/shard_map/jit(_take)/gather | solution.py:51
  36.4 5.4 %gather_fusion.4 = bf16[1536,512]{1,0:T(8,128)(2,1)} fusion(bf16[256,512]{1,0:T(8,128)(2,1)S(1)} %copy-done.2, s32[2048]{0:T(1024)S(1)} %pad_clamp_fusion), kind=kCustom, calls=%fused_computation.1.clone | custom fusion | bytes 3151872 | tf_op jit(solution)/shard_map/jit(_take)/gather | solution.py:51
  41.8 3.3 broadcast_select_fusion
  45.1 4.2 %all-to-all-start.2 = ((bf16[8,192,512]{2,1,0:T(8,128)(2,1)}), bf16[8,192,512]{2,1,0:T(8,128)(2,1)S(1)}, u32[]{:S(2)}, u32[]{:S(2)}) async-start(bf16[8,192,512]{2,1,0:T(8,128)(2,1)} %bitcast.10), calls=%async_computation.2 | async-start | bytes 3145728 | tf_op jit(solution)/shard_map/all_to_all | solution.py:71
  49.3 0.0 all-gather.6.cloned.1.call-start
  49.3 0.7 all-gather.6.cloned.1.call-update
  50.0 20.2 %all-to-all-done.2 = bf16[8,192,512]{2,1,0:T(8,128)(2,1)S(1)} async-done(((bf16[8,192,512]{2,1,0:T(8,128)(2,1)}), bf16[8,192,512]{2,1,0:T(8,128)(2,1)S(1)}, u32[]{:S(2)}, u32[]{:S(2)}) %all-to-all-start.2) | async-done | bytes 1572896 | tf_op jit(solution)/shard_map/all_to_all | solution.py:71
  70.3 4.3 %all-to-all-start.1 = ((bf16[8,192,512]{2,1,0:T(8,128)(2,1)}), bf16[8,192,512]{2,1,0:T(8,128)(2,1)}, u32[]{:S(2)}, u32[]{:S(2)}) async-start(bf16[8,192,512]{2,1,0:T(8,128)(2,1)} %bitcast.4), calls=%async_computation.1 | async-start | bytes 3145728 | tf_op jit(solution)/shard_map/all_to_all | solution.py:72
  74.6 0.2 reduce-scatter.8.cloned.1.call-start
  74.8 0.0 all-gather.8.cloned.1.call-done
  74.8 7.2 %fusion.37 = f32[8,192,1792]{2,1,0:T(8,128)} fusion(bf16[8,192,512]{2,1,0:T(8,128)(2,1)S(1)} %all-to-all-done.2, bf16[1,512,1792]{2,1,0:T(8,128)(2,1)} %all-gather.8.cloned.1.call-done), kind=kOutput, calls=%fused_computation.44 | convolution fusion | flops 2818572288 | bytes 14417920 | tf_op jit(solution)/shard_map/secd,edf->secf/dot_general | solution.py:33
  82.1 13.4 %all-to-all-done.1 = bf16[8,192,512]{2,1,0:T(8,128)(2,1)} async-done(((bf16[8,192,512]{2,1,0:T(8,128)(2,1)}), bf16[8,192,512]{2,1,0:T(8,128)(2,1)}, u32[]{:S(2)}, u32[]{:S(2)}) %all-to-all-start.1) | async-done | bytes 1572896 | tf_op jit(solution)/shard_map/all_to_all | solution.py:72
  95.5 1.7 all-gather.4.cloned.1.call-done
  97.1 9.1 %fusion.43 = f32[8,192,1792]{2,1,0:T(8,128)} fusion(bf16[1,1792,512]{2,1,0:T(8,128)(2,1)} %all-gather.4.cloned.1.call-done, bf16[8,192,512]{2,1,0:T(8,128)(2,1)} %all-to-all-done.1, f32[8,192]{1,0:T(8,128)S(1)} %bitcast.144), kind=kOutput, calls=%fused_computation.50 | convolution fusion | flops 2820931584 | bytes 14424064 | tf_op jit(solution)/shard_map/secd,efd->secf/dot_general | solution.py:40
  106.2 31.8 %all-gather.6.cloned.1.call-done = bf16[1,512,1792]{2,1,0:T(8,128)(2,1)} async-done(((bf16[1,128,1792]{2,1,0:T(8,128)(2,1)}), bf16[1,512,1792]{2,1,0:T(8,128)(2,1)}) %all-gather.6.cloned.1.call-update) | async-done | bytes 1835024 | tf_op jit(solution)/shard_map/all_gather | solution.py:75
  138.0 17.6 %fusion.3 = (bf16[8,1,192,1792]{3,2,0,1:T(8,128)(2,1)}, bf16[8,1,192,1792]{3,2,0,1:T(8,128)(2,1)}, bf16[8,1,192,1792]{3,2,0,1:T(8,128)(2,1)}) fusion(f32[8,192,1792]{2,1,0:T(8,128)} %fusion.37, f32[8,192,1792]{2,1,0:T(8,128)} %fusion.43, bf16[8,192,512]{2,1,0:T(8,128)(2,1)S(1)} %all-to-all-done.2, bf16[1,512,1792]{2,1,0:T(8,128)(2,1)} %all-gather.6.cloned.1.call-done), kind=kOutput, calls=%fused_computation.11 | convolution fusion | flops 2862612480 | bytes 41943040 | tf_op jit(solution)/shard_map/secd,edf->secf/dot_general | solution.py:34
  155.6 8.1 %fusion.28 = f32[1,1792,512]{2,1,0:T(8,128)} fusion(bf16[8,1,192,1792]{3,2,0,1:T(8,128)(2,1)} %get-tuple-element.22, bf16[8,192,512]{2,1,0:T(8,128)(2,1)} %all-to-all-done.1, f32[8,192]{1,0:T(8,128)S(1)} %bitcast.145), kind=kOutput, calls=%fused_computation.38 | convolution fusion | flops 2820931584 | bytes 10754048 | tf_op jit(solution)/shard_map/secf,secd->efd/dot_general | solution.py:46
  163.6 0.0 reduce-scatter.8.cloned.1.call-update
  163.7 0.0 reduce-scatter.6.cloned.1.call-start
  163.7 7.4 %fusion.25 = f32[1,512,1792]{2,1,0:T(8,128)} fusion(bf16[8,192,512]{2,1,0:T(8,128)(2,1)S(1)} %all-to-all-done.2, bf16[8,1,192,1792]{3,2,0,1:T(8,128)(2,1)} %get-tuple-element.24), kind=kOutput, calls=%fused_computation.37 | convolution fusion | flops 2818572288 | bytes 10747904 | tf_op jit(solution)/shard_map/secd,secf->edf/dot_general | solution.py:45
  171.2 0.0 reduce-scatter.6.cloned.1.call-update
  171.2 0.3 reduce-scatter.4.cloned.1.call-start
  171.5 7.4 %fusion.22 = f32[1,512,1792]{2,1,0:T(8,128)} fusion(bf16[8,192,512]{2,1,0:T(8,128)(2,1)S(1)} %all-to-all-done.2, bf16[8,1,192,1792]{3,2,0,1:T(8,128)(2,1)} %get-tuple-element.23), kind=kOutput, calls=%fused_computation.36 | convolution fusion | flops 2818572288 | bytes 10747904 | tf_op jit(solution)/shard_map/secd,secf->edf/dot_general | solution.py:44
  178.9 0.0 reduce-scatter.4.cloned.1.call-update
  178.9 1.5 copy-done.4
  180.4 6.3 %fusion.33 = f32[8,192]{1,0:T(8,128)S(1)} fusion(bf16[8,192,512]{2,1,0:T(8,128)(2,1)} %all-to-all-done.1, bf16[8,1,192,1792]{3,2,0,1:T(8,128)(2,1)} %get-tuple-element.22, bf16[1,1792,512]{2,1,0:T(8,128)(2,1)S(1)} %copy-done.4), kind=kOutput, calls=%fused_computation.41 | convolution fusion | flops 2820930048 | bytes 8919040 | tf_op jit(solution)/shard_map/secf,efd->secd/dot_general | solution.py:36
  186.7 0.6 all_to_all.37
  187.3 3.6 all-to-all-start.4
  191.0 5.7 %fusion.16 = f32[8,192,512]{2,1,0:T(8,128)S(1)} fusion(bf16[8,1,192,1792]{3,2,0,1:T(8,128)(2,1)} %get-tuple-element.24, bf16[1,512,1792]{2,1,0:T(8,128)(2,1)} %all-gather.6.cloned.1.call-done), kind=kOutput, calls=%fused_computation.28 | convolution fusion | flops 2818572288 | bytes 10485760 | tf_op jit(solution)/shard_map/secf,edf->secd/dot_general | solution.py:43
  196.8 4.5 %add_convert_fusion = bf16[8,192,512]{2,1,0:T(8,128)(2,1)} fusion(f32[8,192,512]{2,1,0:T(8,128)S(1)} %fusion.16, bf16[1,512,1792]{2,1,0:T(8,128)(2,1)S(1)} %copy-done.3, bf16[8,1,192,1792]{3,2,0,1:T(8,128)(2,1)S(1)} %bitcast.149), kind=kOutput, calls=%fused_computation.42 | convolution fusion | flops 2820145152 | bytes 12058624 | tf_op jit(solution)/shard_map/secf,edf->secd/dot_general | solution.py:42
  201.2 4.2 %all-to-all-start.3 = ((bf16[8,192,512]{2,1,0:T(8,128)(2,1)}), bf16[8,192,512]{2,1,0:T(8,128)(2,1)S(1)}, u32[]{:S(2)}, u32[]{:S(2)}) async-start(bf16[8,192,512]{2,1,0:T(8,128)(2,1)} %add_convert_fusion), calls=%async_computation.3 | async-start | bytes 3145728 | tf_op jit(solution)/shard_map/all_to_all | solution.py:79
  205.4 0.1 reduce_sum.35
  205.6 0.1 all_to_all.39
  205.7 3.1 gather_fusion.2
  208.8 0.1 gather.26
  209.0 0.1 broadcast_select_fusion.3
  209.0 0.7 copy.22
  209.7 16.7 %all-to-all-done.3 = bf16[8,192,512]{2,1,0:T(8,128)(2,1)S(1)} async-done(((bf16[8,192,512]{2,1,0:T(8,128)(2,1)}), bf16[8,192,512]{2,1,0:T(8,128)(2,1)S(1)}, u32[]{:S(2)}, u32[]{:S(2)}) %all-to-all-start.3) | async-done | bytes 1572896 | tf_op jit(solution)/shard_map/all_to_all | solution.py:79
  226.4 2.0 gather_fusion.1
  228.4 0.2 gather.24
  228.6 2.9 fusion.51
  231.5 71.4 %reduce-scatter.6.cloned.1.call-done = f32[1,128,1792]{2,1,0:T(8,128)} async-done(((f32[1,512,1792]{2,1,0:T(8,128)}), f32[1,128,1792]{2,1,0:T(8,128)}) %reduce-scatter.6.cloned.1.call-update) | async-done | bytes 917520 | tf_op jit(solution)/shard_map/reduce_scatter | solution.py:85
  302.9 71.5 %reduce-scatter.4.cloned.1.call-done = f32[1,128,1792]{2,1,0:T(8,128)} async-done(((f32[1,512,1792]{2,1,0:T(8,128)}), f32[1,128,1792]{2,1,0:T(8,128)}) %reduce-scatter.4.cloned.1.call-update) | async-done | bytes 917520 | tf_op jit(solution)/shard_map/reduce_scatter | solution.py:84
  (28 shorter events, 0.2 us)
Async XLA Ops:
  7.2 24.4 %copy-start = (bf16[256,512]{1,0:T(8,128)(2,1)S(1)}, bf16[256,512]{1,0:T(8,128)(2,1)}, u32[]{:S(2)}) copy-start(bf16[256,512]{1,0:T(8,128)(2,1)} %param.10) | copy-start | bytes 786436
  7.2 67.7 %all-gather.8.cloned.1.call-start = ((), (), s32[]{:S(2)}) async-start(), calls=%async_computation.10 | async-start | bytes 2293760 | tf_op jit(solution)/shard_map/all_gather | solution.py:74
  7.9 89.2 %all-gather.4.cloned.1.call-start = ((), (), s32[]{:S(2)}) async-start(), calls=%async_computation.8 | async-start | bytes 2293760 | tf_op jit(solution)/shard_map/all_gather | solution.py:76
  26.2 18.9 %all-to-all-start = ((f32[8,192,1]{1,2,0:T(1,128)}), f32[8,192,1]{1,2,0:T(1,128)S(1)}, u32[]{:S(2)}, u32[]{:S(2)}) async-start(f32[8,192,1]{1,2,0:T(1,128)} %and_select_fusion), calls=%async_computation | async-start | bytes 16384 | tf_op jit(solution)/shard_map/all_to_all | solution.py:73
  31.6 4.8 %copy-start.2 = (bf16[256,512]{1,0:T(8,128)(2,1)S(1)}, bf16[256,512]{1,0:T(8,128)(2,1)}, u32[]{:S(2)}) copy-start(bf16[256,512]{1,0:T(8,128)(2,1)} %param.9) | copy-start | bytes 786436
  45.1 25.2 %all-to-all-start.2 = ((bf16[8,192,512]{2,1,0:T(8,128)(2,1)}), bf16[8,192,512]{2,1,0:T(8,128)(2,1)S(1)}, u32[]{:S(2)}, u32[]{:S(2)}) async-start(bf16[8,192,512]{2,1,0:T(8,128)(2,1)} %bitcast.10), calls=%async_computation.2 | async-start | bytes 3145728 | tf_op jit(solution)/shard_map/all_to_all | solution.py:71
  49.3 88.7 %all-gather.6.cloned.1.call-start = ((), (), s32[]{:S(2)}) async-start(), calls=%async_computation.9 | async-start | bytes 2293760 | tf_op jit(solution)/shard_map/all_gather | solution.py:75
  70.3 25.2 %all-to-all-start.1 = ((bf16[8,192,512]{2,1,0:T(8,128)(2,1)}), bf16[8,192,512]{2,1,0:T(8,128)(2,1)}, u32[]{:S(2)}, u32[]{:S(2)}) async-start(bf16[8,192,512]{2,1,0:T(8,128)(2,1)} %bitcast.4), calls=%async_computation.1 | async-start | bytes 3145728 | tf_op jit(solution)/shard_map/all_to_all | solution.py:72
  74.6 156.9 %reduce-scatter.8.cloned.1.call-start = ((), (), s32[]{:S(2)}) async-start(), calls=%async_computation.13 | async-start | bytes 4587520 | tf_op jit(solution)/shard_map/reduce_scatter | solution.py:86
  163.7 139.3 %reduce-scatter.6.cloned.1.call-start = ((), (), s32[]{:S(2)}) async-start(), calls=%async_computation.12 | async-start | bytes 4587520 | tf_op jit(solution)/shard_map/reduce_scatter | solution.py:85
  171.2 203.2 %reduce-scatter.4.cloned.1.call-start = ((), (), s32[]{:S(2)}) async-start(), calls=%async_computation.11 | async-start | bytes 4587520 | tf_op jit(solution)/shard_map/reduce_scatter | solution.py:84
  178.9 1.5 copy-start.4
  180.4 16.3 %slice-start = ((s8[5505024]{0:T(1024)(128)(4,1)}), s8[1310720]{0:T(1024)(128)(4,1)S(1)}, s32[]{:S(2)}) async-start(s8[5505024]{0:T(1024)(128)(4,1)} %bitcast.148), calls=%async_computation.14 | async-start | bytes 2621440
  187.3 13.9 %all-to-all-start.4 = ((f32[8,192,1]{1,2,0:T(1,128)}), f32[8,192,1]{1,2,0:T(1,128)S(1)}, u32[]{:S(2)}, u32[]{:S(2)}) async-start(f32[8,192,1]{1,2,0:T(1,128)} %all_to_all.37), calls=%async_computation.4 | async-start | bytes 16384 | tf_op jit(solution)/shard_map/all_to_all | solution.py:80
  191.0 5.8 %copy-start.3 = (bf16[1,512,1792]{2,1,0:T(8,128)(2,1)S(1)}, bf16[1,512,1792]{2,1,0:T(8,128)(2,1)}, u32[]{:S(2)}) copy-start(bf16[1,512,1792]{2,1,0:T(8,128)(2,1)} %all-gather.8.cloned.1.call-done) | copy-start | bytes 5505028
  191.0 5.8 %slice-start.1 = ((s8[5505024]{0:T(1024)(128)(4,1)}), s8[4194304]{0:T(1024)(128)(4,1)S(1)}, s32[]{:S(2)}) async-start(s8[5505024]{0:T(1024)(128)(4,1)} %bitcast.148), calls=%async_computation.15 | async-start | bytes 8388608
  201.2 25.2 %all-to-all-start.3 = ((bf16[8,192,512]{2,1,0:T(8,128)(2,1)}), bf16[8,192,512]{2,1,0:T(8,128)(2,1)S(1)}, u32[]{:S(2)}, u32[]{:S(2)}) async-start(bf16[8,192,512]{2,1,0:T(8,128)(2,1)} %add_convert_fusion), calls=%async_computation.3 | async-start | bytes 3145728 | tf_op jit(solution)/shard_map/all_to_all | solution.py:79
  226.4 148.0 %copy-start.1 = (bf16[256,512]{1,0:T(8,128)(2,1)S(1)}, bf16[256,512]{1,0:T(8,128)(2,1)}, u32[]{:S(2)}) copy-start(bf16[256,512]{1,0:T(8,128)(2,1)} %param.10) | copy-start | bytes 786436
Sparse Core Ops, SparseCore 0:
  9.6 43.7 all-gather.7
  54.9 42.2 all-gather.3
  98.7 39.2 all-gather.5
  163.8 67.6 reduce-scatter.7
  234.2 68.6 reduce-scatter.5
  305.7 68.6 reduce-scatter.3
where the time goes:
time: 382 us; the launch traced here: 381 us
  waiting for transfers between devices  229 us (60%)
  matrix products  73.3 us (19%)
  local copies, waits for them, and re-layouts  30.7 us (8%)
  starting transfers between devices  22.3 us (6%)
  between operations  14.4 us (4%)
  other arithmetic  11.7 us (3%)
    reduce_scatter x1, waiting for transfers between devices, per_device(): lax.psum_scatter(dw_gate, 'fsdp', scatter_dimension=1, tiled=True)  71.5 us
    reduce_scatter x1, waiting for transfers between devices, per_device(): grad_w_up = lax.psum_scatter(dw_up, 'fsdp', scatter_dimension=1, tiled=True)  71.4 us
    all_gather x1, waiting for transfers between devices, per_device(): w_up_full = lax.all_gather(w_up, 'fsdp', axis=1, tiled=True)  31.8 us
    gather x8, local copies, waits for them, and re-layouts, take_rows(): return jnp.take(rows, row_ids, axis=0, mode='fill', fill_value=0)  25.2 us
    all_to_all x1, waiting for transfers between devices, per_device(): lax.all_to_all(x_send, 'ep', 0, 0, tiled=True)  20.2 us
    dot_general x1, matrix products, expert_backward(): jnp.einsum('secd,edf->secf', x_rows, w_up_full, preferred_element_type=jn...  17.6 us
    all_to_all x1, waiting for transfers between devices, per_device(): lax.all_to_all(dx_rows.reshape(n_ep * exp_local * capacity, d_model), 'ep...  16.7 us
    all_to_all x1, waiting for transfers between devices, per_device(): lax.all_to_all(dy_send, 'ep', 0, 0, tiled=True)  13.4 us
  transfers between devices with their start and end apart: 11, of which 7 were waited for; matrix products, arithmetic and copies ran while one was open for 23% of the time, Pallas kernels for 0%

commit v1 on v0

v1 whole, which is shorter than its diff:
```python
import functools

import jax
import jax.numpy as jnp
from jax import lax
from jax.experimental import pallas as pl
from jax.experimental.pallas import tpu as pltpu
from jax.sharding import PartitionSpec as P

MESH = pl.DeviceIdType.MESH
CAP_FACTOR = 3
CHUNKS = 7
F32 = jnp.float32
BF16 = jnp.bfloat16
DIAG = (2, 4, 6)
DIRECT = (1, 2, 4, 6)
B_SLOT = (2, 3, 5, 7)
C_SLOT = (3, 4, 6, 8)


def capacity_of(tok_dev, top_k, experts):
    return max(8, ((CAP_FACTOR * tok_dev * top_k // experts + 7) // 8) * 8)


def flip(p, q):
    for b in (1, 2, 4):
        if q & b:
            p = p + b - 2 * b * lax.rem(lax.div(p, b), 2)
    return p


def dot_nn(a, b):
    return jnp.dot(a, b, preferred_element_type=F32)


def dot_nt(a, b):
    return lax.dot_general(a, b, (((1,), (1,)), ((), ())), preferred_element_type=F32)


def dot_tn(a, b):
    return lax.dot_general(a, b, (((0,), (0,)), ((), ())), preferred_element_type=F32)


def iota_f32(shape, dim):
    return lax.broadcasted_iota(jnp.int32, shape, dim).astype(F32)


def positions(meta, tri, cap):
    ids0, ids1 = meta[0:1, :], meta[1:2, :]
    row = iota_f32((16, meta.shape[1]), 0)
    chosen = jnp.where(ids0 == row, 1.0, 0.0) + jnp.where(ids1 == row, 1.0, 0.0)
    before = dot_nn(chosen.astype(BF16), tri)
    return jnp.where((chosen > 0.0) & (before < cap), before, -1.0)


def pick_row(pos16, e):
    row = iota_f32(pos16.shape, 0)
    return jnp.sum(jnp.where(row == e, pos16, 0.0), axis=0, keepdims=True)


def kernel(cap, n_z, n_p, meta_ref, xd_ref, w_ref, gx_ref, dr_ref, dw0_ref, dw1_ref, dw2_ref,
           xd_all, meta_all, w_all, tri_ref, xc_ref, gc_ref, dyc_ref, xt_ref, gt_ref, y_ref, dx_ref,
           dxs_ref, dxr_ref, drs_ref, drr_ref, gxa_ref,
           s_zt, r_zt, s_zm, r_zm, s_w, r_w, s_p, r_p, s_pm, r_pm, s_r, s_rm,
           s_dx, r_dx, s_dr, r_dr, s_loc):
    z = lax.axis_index("fsdp")
    p = lax.axis_index("ep")
    e_mine = p.astype(F32)
    n_tok, d2 = xd_ref.shape
    d = d2 // 2
    dl = w_ref.shape[1]
    f = w_ref.shape[2]
    fc = f // CHUNKS
    per_h = 4
    n_h = n_p // per_h
    partner = flip(p, 1)

    def plane_of(o):
        m = lax.div(z, 2)
        zz = z + m * (3 - 2 * z)
        if isinstance(o, int):
            jj = (zz, 1 - zz, 2, 3)[o]
        else:
            jj = o + jnp.where(o < 2, zz * (1 - 2 * o), 0)
        return jj + m * (3 - 2 * jj)

    barrier = pltpu.get_barrier_semaphore()
    for q in range(1, n_p):
        pl.semaphore_signal(barrier, inc=1, device_id={"ep": flip(p, q)}, device_id_type=MESH)
    for step in (1, -1):
        nb = z + step

        @pl.when((nb >= 0) & (nb < n_z))
        def _():
            pl.semaphore_signal(barrier, inc=1, device_id={"fsdp": nb}, device_id_type=MESH)

    inner = jnp.where(z > 0, 1, 0) + jnp.where(z < n_z - 1, 1, 0)
    pl.semaphore_wait(barrier, n_p - 1 + inner)

    def remote(src, dst, ssem, rsem, dev):
        return pltpu.make_async_remote_copy(
            src_ref=src, dst_ref=dst, send_sem=ssem, recv_sem=rsem, device_id=dev, device_id_type=MESH)

    def w_block(j, c):
        return w_all.at[:, pl.ds(pl.multiple_of(j * dl, dl), dl), pl.ds(pl.multiple_of(c * fc, fc), fc)]

    def zt_copy(j, way, own):
        dev = {"fsdp": z + 1 - 2 * way}
        return (remote(xd_ref if own else xd_all.at[j, p], xd_all.at[j, p], s_zt.at[way, j], r_zt.at[j], dev),
                remote(meta_ref if own else meta_all.at[j, p], meta_all.at[j, p], s_zm.at[way, j], r_zm.at[j], dev))

    def w_copy(j, c, way, own):
        src = w_ref.at[:, :, pl.ds(pl.multiple_of(c * fc, fc), fc)] if own else w_block(j, c)
        return remote(src, w_block(j, c), s_w.at[way, j, c], r_w.at[j, c], {"fsdp": z + 1 - 2 * way})

    def plane_copy(j, i, own):
        dev = {"ep": flip(p, DIRECT[i])}
        return (remote(xd_ref if own else xd_all.at[j, p], xd_all.at[j, p], s_p.at[j, i], r_p.at[j, p], dev),
                remote(meta_ref if own else meta_all.at[j, p], meta_all.at[j, p], s_pm.at[j, i], r_pm.at[j, p], dev))

    def relay_copy(j, i):
        pp = flip(p, DIAG[i])
        dev = {"ep": partner}
        return (remote(xd_all.at[j, pp], xd_all.at[j, pp], s_r.at[j, i], r_p.at[j, pp], dev),
                remote(meta_all.at[j, pp], meta_all.at[j, pp], s_rm.at[j, i], r_pm.at[j, pp], dev))

    def plane_wait(j, pp):
        remote(xd_all.at[j, pp], xd_all.at[j, pp], s_p.at[j, 0], r_p.at[j, pp], {"ep": partner}).wait_recv()
        remote(meta_all.at[j, pp], meta_all.at[j, pp], s_pm.at[j, 0], r_pm.at[j, pp], {"ep": partner}).wait_recv()

    def valid_z(j):
        return (j >= 0) & (j < n_z)

    def start_all(copies):
        for c in copies:
            c.start()

    for way in (0, 1):
        @pl.when(valid_z(z + 1 - 2 * way))
        def _():
            start_all(zt_copy(z, way, True))
    for i in range(4):
        start_all(plane_copy(z, i, True))
    loc_x = pltpu.make_async_copy(xd_ref, xd_all.at[z, p], s_loc.at[0])
    loc_m = pltpu.make_async_copy(meta_ref, meta_all.at[z, p], s_loc.at[1])
    loc_w = pltpu.make_async_copy(
        w_ref, w_all.at[:, pl.ds(pl.multiple_of(z * dl, dl), dl), :], s_loc.at[2])
    loc_x.start()
    loc_m.start()
    loc_w.start()

    tri_ref[...] = jnp.where(iota_f32((n_tok, n_tok), 0) < iota_f32((n_tok, n_tok), 1), 1.0, 0.0).astype(BF16)
    for ref in (dw0_ref, dw1_ref, dw2_ref, y_ref, dx_ref):
        ref[...] = jnp.zeros_like(ref)
    loc_x.wait()
    loc_m.wait()
    loc_w.wait()

    def rows_of(s):
        return lax.div(s, per_h), pl.ds(pl.multiple_of(lax.rem(s, per_h) * cap, cap), cap)

    def compact(o, j):
        def one(s, carry):
            meta = meta_all[j, s]
            pos = pick_row(positions(meta, tri_ref[...], cap), e_mine)
            hit = iota_f32((cap, n_tok), 0) == pos
            r_row = (jnp.where(meta[0:1, :] == e_mine, meta[2:3, :], 0.0)
                     + jnp.where(meta[1:2, :] == e_mine, meta[3:4, :], 0.0))
            r_col = jnp.sum(jnp.where(hit, r_row, 0.0), axis=1, keepdims=True)
            got = dot_nn(jnp.where(hit, 1.0, 0.0).astype(BF16), xd_all[j, s])
            h, rows = rows_of(s)
            dy = got[:, d:]
            xc_ref[o * n_h + h, rows, :] = got[:, :d].astype(BF16)
            gc_ref[o * n_h + h, rows, :] = (r_col * dy).astype(BF16)

            @pl.when(o == 0)
            def _():
                dyc_ref[h, rows, :] = dy.astype(BF16)

            return carry

        lax.fori_loop(0, n_p, one, 0)

        def turn(h, carry):
            cols = pl.ds(pl.multiple_of(z * dl, dl), dl)
            xt_ref[o * n_h + h] = xc_ref[o * n_h + h, :, cols].T
            gt_ref[o * n_h + h] = gc_ref[o * n_h + h, :, cols].T
            return carry

        lax.fori_loop(0, n_h, turn, 0)

    def cell(o, c, h):
        i = o * n_h + h
        cols = pl.ds(pl.multiple_of(c * fc, fc), fc)
        x, g = xc_ref[i], gc_ref[i]
        w1, w3, w2 = w_all[0, :, cols], w_all[1, :, cols], w_all[2, :, cols]
        h1 = dot_nn(x, w1)
        h3 = dot_nn(x, w3)
        da = dot_nn(g, w2)
        s = jax.nn.sigmoid(h1)
        a = (h1 * s * h3).astype(BF16)
        t = da * s
        dh3 = (t * h1).astype(BF16)
        dh1 = (t * h3 * (1.0 + h1 * (1.0 - s))).astype(BF16)
        dw0_ref[:, cols] += dot_nn(xt_ref[i], dh1)
        dw1_ref[:, cols] += dot_nn(xt_ref[i], dh3)
        dw2_ref[:, cols] += dot_nn(gt_ref[i], a)

        @pl.when(o == 0)
        def _():
            y_ref[h] += dot_nt(a, w2)
            dx_ref[h] += dot_nt(dh1, w1) + dot_nt(dh3, w3)

    def send_back():
        def one(s, carry):
            h, rows = rows_of(s)
            dxs_ref[s] = dx_ref[h, rows, :].astype(BF16)
            dr_col = jnp.sum(dyc_ref[h, rows, :].astype(F32) * y_ref[h, rows, :], axis=1, keepdims=True)
            pos = pick_row(positions(meta_all[z, s], tri_ref[...], cap), e_mine)
            hit = iota_f32((cap, n_tok), 0) == pos
            dr_row = jnp.sum(jnp.where(hit, dr_col, 0.0), axis=0, keepdims=True)
            drs_ref[s] = jnp.broadcast_to(dr_row, (8, n_tok))
            return carry

        lax.fori_loop(0, n_p, one, 0)
        for q in range(1, n_p):
            start_all(back_copy(q))
        for c in own_back():
            c.start()

    def back_copy(q):
        to = flip(p, q)
        return (remote(dxs_ref.at[to], dxr_ref.at[p], s_dx.at[q], r_dx.at[p], {"ep": to}),
                remote(drs_ref.at[to], drr_ref.at[p], s_dr.at[q], r_dr.at[p], {"ep": to}))

    def own_back():
        return (pltpu.make_async_copy(dxs_ref.at[p], dxr_ref.at[p], s_dx.at[0]),
                pltpu.make_async_copy(drs_ref.at[p], drr_ref.at[p], s_dr.at[0]))

    last = CHUNKS + 3

    def slot(k, carry):
        @pl.when(k < n_z)
        def _():
            for way in (0, 1):
                j = z - k * (1 - 2 * way)

                @pl.when(valid_z(j))
                def _():
                    for c in zt_copy(j, way, False):
                        c.wait_recv()

                    @pl.when(valid_z(z + 1 - 2 * way))
                    def _():
                        start_all(zt_copy(j, way, False))

                    for i in range(4):
                        start_all(plane_copy(j, i, False))

        for dist in (2, 1, 3):
            c = k - 1 - dist
            for way in (0, 1):
                j = z - dist * (1 - 2 * way)

                @pl.when(valid_z(j) & (c >= 0) & (c < CHUNKS))
                def _():
                    w_copy(j, c, way, False).wait_recv()

                    @pl.when(valid_z(z + 1 - 2 * way))
                    def _():
                        w_copy(j, c, way, False).start()

        for way in (0, 1):
            @pl.when(valid_z(z + 1 - 2 * way) & (k - 1 < CHUNKS))
            def _():
                w_copy(z, k - 1, way, True).start()

        for o in range(4):
            @pl.when(k == B_SLOT[o])
            def _():
                j = plane_of(o)
                for q in DIAG:
                    plane_wait(j, flip(p, q))
                for i in range(3):
                    start_all(relay_copy(j, i))

        def plane(o, carry):
            at = 3 + o + lax.div(o, 2) + lax.div(o, 3)

            @pl.when(k == at)
            def _():
                j = plane_of(o)
                plane_wait(j, partner)
                for q in DIAG:
                    plane_wait(j, flip(partner, q))
                compact(o, j)

            lo = jnp.where(k == at, 0, jnp.maximum(k - 4, 0))
            hi = jnp.where(k < at, lo, jnp.maximum(k - 3, 0))

            def chunk(c, carry):
                def half(h, carry):
                    cell(o, c, h)
                    return carry

                return lax.fori_loop(0, n_h, half, carry)

            lax.fori_loop(lo, hi, chunk, 0)

            @pl.when((o == 0) & (k == last))
            def _():
                send_back()

            return carry

        return lax.fori_loop(0, n_z, plane, carry)

    lax.fori_loop(1, last + 1, slot, 0)

    for q in range(1, n_p):
        frm = flip(p, q)
        remote(dxs_ref.at[frm], dxr_ref.at[frm], s_dx.at[q], r_dx.at[frm], {"ep": frm}).wait_recv()
        remote(drs_ref.at[frm], drr_ref.at[frm], s_dr.at[q], r_dr.at[frm], {"ep": frm}).wait_recv()
    for c in own_back():
        c.wait()
    meta = meta_ref[...]
    pos16 = positions(meta, tri_ref[...], cap)
    gxa_ref[...] = jnp.zeros_like(gxa_ref)
    dr_ref[...] = jnp.zeros_like(dr_ref)

    def gather(e, carry):
        ef = e.astype(F32)
        pos = pick_row(pos16, ef)
        hit = jnp.where(iota_f32((cap, n_tok), 0) == pos, 1.0, 0.0).astype(BF16)
        gxa_ref[...] += dot_tn(hit, dxr_ref[e])
        dr = drr_ref[e]
        for j in range(2):
            dr_ref[j:j + 1, :] += jnp.where(meta[j:j + 1, :] == ef, dr[0:1, :], 0.0)
        return carry

    lax.fori_loop(0, n_p, gather, 0)
    gx_ref[...] = gxa_ref[...].astype(BF16)

    for q in range(1, n_p):
        for c in back_copy(q):
            c.wait_send()
    for i in range(4):
        for j in range(n_z):
            for c in plane_copy(j, i, False):
                c.wait_send()
    for i in range(3):
        for j in range(n_z):
            for c in relay_copy(j, i):
                c.wait_send()
    for way in (0, 1):
        for dist in range(n_z):
            j = z - dist * (1 - 2 * way)

            @pl.when(valid_z(j) & valid_z(z + 1 - 2 * way))
            def _():
                for c in zt_copy(j, way, False):
                    c.wait_send()

                def drain(c, carry):
                    w_copy(j, c, way, False).wait_send()
                    return carry

                lax.fori_loop(0, CHUNKS, drain, 0)


def solution(mesh):
    n_z, n_p = mesh.shape["fsdp"], mesh.shape["ep"]
    tok_spec = P(("fsdp", "ep"), None)
    spec_in = P("ep", "fsdp", None)
    spec_out = P("ep", None, "fsdp")

    def per_device(x_tok, dy_tok, expert_ids, route_w, w_gate, w_up, w_down):
        n_tok, top_k = expert_ids.shape
        d = x_tok.shape[1]
        dl, f = w_gate.shape[1], w_gate.shape[2]
        cap = capacity_of(n_tok, top_k, n_p)
        xd = jnp.concatenate([x_tok, dy_tok], axis=1)
        meta = jnp.concatenate(
            [expert_ids.astype(F32).T, route_w.T, jnp.zeros((4, n_tok), F32)], axis=0)
        w = jnp.stack([w_gate[0], w_up[0], w_down[0].T])
        rows = 4 * cap
        n_t = n_z * n_p // 4
        sem = pltpu.SemaphoreType.DMA
        vmem = pl.BlockSpec(memory_space=pltpu.VMEM)
        out = jax.ShapeDtypeStruct
        gx, dr, dw0, dw1, dw2 = pl.pallas_call(
            functools.partial(kernel, cap, n_z, n_p),
            out_shape=(out((n_tok, d), BF16), out((8, n_tok), F32),
                       out((dl, f), F32), out((dl, f), F32), out((dl, f), F32)),
            in_specs=[vmem] * 3,
            out_specs=(vmem,) * 5,
            scratch_shapes=[
                pltpu.VMEM((n_z, n_p, n_tok, 2 * d), BF16),
                pltpu.VMEM((n_z, n_p, 8, n_tok), F32),
                pltpu.VMEM((3, n_z * dl, f), BF16),
                pltpu.VMEM((n_tok, n_tok), BF16),
                pltpu.VMEM((n_t, rows, d), BF16),
                pltpu.VMEM((n_t, rows, d), BF16),
                pltpu.VMEM((n_p // 4, rows, d), BF16),
                pltpu.VMEM((n_t, dl, rows), BF16),
                pltpu.VMEM((n_t, dl, rows), BF16),
                pltpu.VMEM((n_p // 4, rows, d), F32),
                pltpu.VMEM((n_p // 4, rows, d), F32),
                pltpu.VMEM((n_p, cap, d), BF16),
                pltpu.VMEM((n_p, cap, d), BF16),
                pltpu.VMEM((n_p, 8, n_tok), F32),
                pltpu.VMEM((n_p, 8, n_tok), F32),
                pltpu.VMEM((n_tok, d), F32),
                sem((2, n_z)), sem((n_z,)), sem((2, n_z)), sem((n_z,)),
                sem((2, n_z, CHUNKS)), sem((n_z, CHUNKS)),
                sem((n_z, 4)), sem((n_z, n_p)), sem((n_z, 4)), sem((n_z, n_p)),
                sem((n_z, 3)), sem((n_z, 3)),
                sem((n_p,)), sem((n_p,)), sem((n_p,)), sem((n_p,)),
                sem((3,)),
            ],
            compiler_params=pltpu.CompilerParams(
                collective_id=0, has_side_effects=True, vmem_limit_bytes=67043328),
        )(meta, xd, w)
        return gx, dr[:top_k].T, dw0[None], dw1[None], dw2.T[None]

    return jax.shard_map(
        per_device, mesh=mesh,
        in_specs=(tok_spec, tok_spec, tok_spec, tok_spec, spec_in, spec_in, spec_out),
        out_specs=(tok_spec, tok_spec, spec_in, spec_in, spec_out),
        check_vma=False)
```

time: 382 us -> 219 us (0.57)
  the two profiles are of different devices: /device:TPU:0 before, /device:TPU:25 now
where the time goes in v1:
time: 219 us
  Pallas kernels  205 us (94%)
  local copies, waits for them, and re-layouts  7.64 us (3%)
  other arithmetic  5.22 us (2%)
    pallas_call x1, Pallas kernels, per_device(): pl.pallas_call(functools.partial(kernel, cap, n_z, n_p), out_shape=(out((...  205 us
    unnamed x15, local copies, waits for them, and re-layouts  6.19 us

profile of v1, /device:TPU:25, one launch (start us, length us, event | category | flops | bytes accessed | tf_op | source)
XLA Modules:
  0.0 218.7 jit_solution(15611792814631362698)
XLA Ops:
  0.6 0.0 copy-start.2
  0.6 0.0 copy-start.3
  0.7 0.1 pad.7.clone
  0.7 0.7 convert_bitcast_fusion
  1.5 1.3 maximum_maximum_fusion.meta_ref
  2.8 1.2 copy.12
  4.1 1.9 pad_maximum_fusion.1.xd_ref
  5.9 0.0 copy-done.2
  5.9 0.0 copy-done.3
  5.9 1.3 pad_maximum_fusion.w_ref
  7.2 205.1 %shard_map.110 = (bf16[256,512]{1,0:T(8,128)(2,1)}, f32[8,256]{1,0:T(8,128)}, f32[128,1792]{1,0:T(8,128)}, f32[128,1792]{1,0:T(8,128)}, f32[128,1792]{1,0:T(8,128)}) custom-call(f32[8,256]{1,0:T(8,128)} %maximum_maximum_fusion.meta_ref, bf16[256,1024]{1,0:T(8,128)(2,1)} %pad_maximum_fusion.1.xd_ref, bf16[3,128,1792]{2,1,0:T(8,128)(2,1)} %pad_maximum_fusion.w_ref), custom_call_target="tpu_custom_call" | custom-call | tf_op jit(solution)/shard_map/pallas_call | solution.py:391
  212.3 0.0 copy-start.4
  212.3 0.0 copy-start.1
  212.3 1.4 slice_bitcast_fusion
  213.7 2.4 %copy.13 = f32[1,1792,128]{2,1,0:T(8,128)} copy(f32[1,1792,128]{1,2,0:T(8,128)} %bitcast.18) | data formatting | bytes 1835008
  216.1 0.0 copy-done.4
  216.1 0.0 copy-start
  216.1 0.7 copy.17
  216.8 0.0 copy-done.1
  216.8 0.9 copy.18
  217.7 0.0 copy-done
  217.7 0.9 copy.19
  (1 shorter events, 0.0 us)
Async XLA Ops:
  0.6 5.3 %copy-start.2 = (bf16[1,128,1792]{2,1,0:T(8,128)(2,1)S(1)}, bf16[1,128,1792]{2,1,0:T(8,128)(2,1)}, u32[]{:S(2)}) copy-start(bf16[1,128,1792]{2,1,0:T(8,128)(2,1)} %param.12) | copy-start | bytes 1376260
  0.6 5.3 %copy-start.3 = (bf16[1,128,1792]{2,1,0:T(8,128)(2,1)S(1)}, bf16[1,128,1792]{2,1,0:T(8,128)(2,1)}, u32[]{:S(2)}) copy-start(bf16[1,128,1792]{2,1,0:T(8,128)(2,1)} %param.11) | copy-start | bytes 1376260
  212.3 3.8 %copy-start.4 = (bf16[256,512]{1,0:T(8,128)(2,1)S(1)}, bf16[256,512]{1,0:T(8,128)(2,1)}, u32[]{:S(2)}) copy-start(bf16[256,512]{1,0:T(8,128)(2,1)} %get-tuple-element.25) | copy-start | bytes 786436
  212.3 4.5 %copy-start.1 = (f32[128,1792]{1,0:T(8,128)S(1)}, f32[128,1792]{1,0:T(8,128)}, u32[]{:S(2)}) copy-start(f32[128,1792]{1,0:T(8,128)} %get-tuple-element.12) | copy-start | bytes 2752516
  216.1 1.6 copy-start

commit v2 on v1

v2 whole, which is shorter than its diff:
```python
import functools

import jax
import jax.numpy as jnp
from jax import lax
from jax.experimental import pallas as pl
from jax.experimental.pallas import tpu as pltpu
from jax.sharding import PartitionSpec as P

MESH = pl.DeviceIdType.MESH
CAP_FACTOR = 3
CHUNKS = 7
F32 = jnp.float32
BF16 = jnp.bfloat16
DIAG = (2, 4, 6)
DIRECT = (1, 2, 4, 6)
SUB = 3
ORDER = ((0, 1, 2, 3), (1, 0, 2, 3), (2, 1, 3, 0), (3, 2, 1, 0))
STEPS = (
    (0, (0, 0), (0, 0), (0, 0), (0, 0)),
    (-1, (0, 1), (0, 0), (0, 0), (0, 0)),
    (1, (0, 0), (0, 1), (0, 0), (0, 0)),
    (-1, (1, 2), (1, 2), (0, 0), (0, 0)),
    (2, (0, 0), (0, 0), (0, 2), (0, 0)),
    (-1, (2, 3), (2, 3), (2, 3), (0, 0)),
    (-1, (3, 4), (3, 4), (3, 4), (0, 0)),
    (3, (0, 0), (0, 0), (0, 0), (0, 4)),
    (-1, (4, 5), (4, 5), (4, 5), (4, 5)),
    (-1, (5, 6), (5, 6), (5, 6), (5, 6)),
    (-1, (6, 7), (6, 7), (6, 7), (6, 7)),
)


def capacity_of(tok_dev, top_k, experts):
    return max(8, ((CAP_FACTOR * tok_dev * top_k // experts + 7) // 8) * 8)


def flip(p, q):
    for b in (1, 2, 4):
        if q & b:
            p = p + b - 2 * b * lax.rem(lax.div(p, b), 2)
    return p


def dot_nn(a, b):
    return jnp.dot(a, b, preferred_element_type=F32)


def dot_nt(a, b):
    return lax.dot_general(a, b, (((1,), (1,)), ((), ())), preferred_element_type=F32)


def dot_tn(a, b):
    return lax.dot_general(a, b, (((0,), (0,)), ((), ())), preferred_element_type=F32)


def iota_f32(shape, dim):
    return lax.broadcasted_iota(jnp.int32, shape, dim).astype(F32)


def positions(meta, tri, cap):
    ids0, ids1 = meta[0:1, :], meta[1:2, :]
    row = iota_f32((16, meta.shape[1]), 0)
    chosen = jnp.where(ids0 == row, 1.0, 0.0) + jnp.where(ids1 == row, 1.0, 0.0)
    before = dot_nn(chosen.astype(BF16), tri)
    return jnp.where((chosen > 0.0) & (before < cap), before, -1.0)


def pick_row(pos16, e):
    row = iota_f32(pos16.shape, 0)
    return jnp.sum(jnp.where(row == e, pos16, 0.0), axis=0, keepdims=True)


def pick(table, i):
    return sum(jnp.where(i == n, v, 0) for n, v in enumerate(table))


def kernel(cap, n_z, n_p, ids_ref, rw_ref, x_ref, dy_ref, wg_ref, wu_ref, wd_ref,
           gx_ref, dr_ref, dw0_ref, dw1_ref, dw2_ref,
           xd_all, meta_all, w_all, tri_ref, xc_ref, gc_ref, dyc_ref, xt_ref, gt_ref, y_ref, dx_ref,
           dxs_ref, dxr_ref, drs_ref, drr_ref, gxa_ref, dwt_ref,
           s_zt, r_zt, s_zm, r_zm, s_w, r_w, s_p, r_p, s_pm, r_pm, s_r, s_rm,
           s_dx, r_dx, s_dr, r_dr, s_loc):
    z = lax.axis_index("fsdp")
    p = lax.axis_index("ep")
    e_mine = p.astype(F32)
    n_tok, d = x_ref.shape
    dl, f = wg_ref.shape[1:]
    fc = f // CHUNKS
    per_h = 4
    n_h = n_p // per_h
    partner = flip(p, 1)
    own_rows = pl.ds(pl.multiple_of(z * dl, dl), dl)

    def plane_of(o):
        if isinstance(o, int):
            return pick([t[o] for t in ORDER], z)
        return sum(jnp.where(z == n, pick(t, o), 0) for n, t in enumerate(ORDER))

    loads = (
        pltpu.make_async_copy(x_ref, xd_all.at[z, p, :, pl.ds(0, d)], s_loc.at[0]),
        pltpu.make_async_copy(dy_ref, xd_all.at[z, p, :, pl.ds(d, d)], s_loc.at[1]),
        pltpu.make_async_copy(wg_ref.at[0], w_all.at[0, own_rows, :], s_loc.at[2]),
        pltpu.make_async_copy(wu_ref.at[0], w_all.at[1, own_rows, :], s_loc.at[3]),
    )
    for c in loads:
        c.start()

    barrier = pltpu.get_barrier_semaphore()
    for q in range(1, n_p):
        pl.semaphore_signal(barrier, inc=1, device_id={"ep": flip(p, q)}, device_id_type=MESH)
    for step in (1, -1):
        nb = z + step

        @pl.when((nb >= 0) & (nb < n_z))
        def _():
            pl.semaphore_signal(barrier, inc=1, device_id={"fsdp": nb}, device_id_type=MESH)

    for c in range(CHUNKS):
        w_all[2, own_rows, c * fc:(c + 1) * fc] = wd_ref[0, c * fc:(c + 1) * fc, :].T
    meta_all[z, p, 0:2, :] = ids_ref[...].astype(F32)
    meta_all[z, p, 2:4, :] = rw_ref[...]
    meta_all[z, p, 4:8, :] = jnp.zeros((4, n_tok), F32)
    tri_ref[...] = jnp.where(iota_f32((n_tok, n_tok), 0) < iota_f32((n_tok, n_tok), 1), 1.0, 0.0).astype(BF16)
    for ref in (dw0_ref, dw1_ref, dwt_ref, y_ref, dx_ref):
        ref[...] = jnp.zeros_like(ref)
    for c in loads:
        c.wait()
    inner = jnp.where(z > 0, 1, 0) + jnp.where(z < n_z - 1, 1, 0)
    pl.semaphore_wait(barrier, n_p - 1 + inner)

    def remote(src, dst, ssem, rsem, dev):
        return pltpu.make_async_remote_copy(
            src_ref=src, dst_ref=dst, send_sem=ssem, recv_sem=rsem, device_id=dev, device_id_type=MESH)

    def w_block(j, c):
        return w_all.at[:, pl.ds(pl.multiple_of(j * dl, dl), dl), pl.ds(pl.multiple_of(c * fc, fc), fc)]

    def zt_copy(j, way):
        dev = {"fsdp": z + 1 - 2 * way}
        return (remote(meta_all.at[j, p], meta_all.at[j, p], s_zm.at[way, j], r_zm.at[j], dev),
                remote(xd_all.at[j, p], xd_all.at[j, p], s_zt.at[way, j], r_zt.at[j], dev))

    def w_copy(j, c, way):
        return remote(w_block(j, c), w_block(j, c), s_w.at[way, j, c], r_w.at[j, c], {"fsdp": z + 1 - 2 * way})

    def plane_copy(j, i):
        dev = {"ep": flip(p, DIRECT[i])}
        return (remote(meta_all.at[j, p], meta_all.at[j, p], s_pm.at[j, i], r_pm.at[j, p], dev),
                remote(xd_all.at[j, p], xd_all.at[j, p], s_p.at[j, i], r_p.at[j, p], dev))

    def relay_copy(j, i):
        pp = flip(p, DIAG[i])
        dev = {"ep": partner}
        return (remote(meta_all.at[j, pp], meta_all.at[j, pp], s_rm.at[j, i], r_pm.at[j, pp], dev),
                remote(xd_all.at[j, pp], xd_all.at[j, pp], s_r.at[j, i], r_p.at[j, pp], dev))

    def plane_wait(j, pp):
        remote(meta_all.at[j, pp], meta_all.at[j, pp], s_pm.at[j, 0], r_pm.at[j, pp], {"ep": partner}).wait_recv()
        remote(xd_all.at[j, pp], xd_all.at[j, pp], s_p.at[j, 0], r_p.at[j, pp], {"ep": partner}).wait_recv()

    def valid_z(j):
        return (j >= 0) & (j < n_z)

    def start_all(copies):
        for c in copies:
            c.start()

    def link(way):
        return valid_z(z + 1 - 2 * way), (z if way == 0 else n_z - 1 - z)

    def upstream(way, dist):
        return z - dist * (1 - 2 * way)

    def own_w(depths, chunks):
        for way in (0, 1):
            there, depth = link(way)
            for q in depths:
                @pl.when(there & (depth == q))
                def _():
                    for c in chunks:
                        w_copy(z, c, way).start()

    def pass_w(q, dist, c):
        for way in (0, 1):
            there, depth = link(way)

            @pl.when(there & (depth == q))
            def _():
                j = upstream(way, dist)
                w_copy(j, c, way).wait_recv()
                w_copy(j, c, way).start()

    def need_w(c):
        for way in (0, 1):
            there, _ = link(way)
            for dist in range(1, n_z):
                j = upstream(way, dist)

                @pl.when(jnp.logical_not(there) & valid_z(j))
                def _():
                    w_copy(j, c, way).wait_recv()

    def tokens(dist):
        for way in (0, 1):
            there, _ = link(way)
            j = upstream(way, dist)

            @pl.when(valid_z(j))
            def _():
                for c in zt_copy(j, way):
                    c.wait_recv()

                @pl.when(there)
                def _():
                    start_all(zt_copy(j, way))

                for i in range(4):
                    start_all(plane_copy(j, i))

    def relay(o):
        j = plane_of(o)
        for i, q in enumerate(DIAG):
            plane_wait(j, flip(p, q))
            start_all(relay_copy(j, i))

    def landed(j):
        plane_wait(j, partner)
        for q in DIAG:
            plane_wait(j, flip(partner, q))

    def batch(q, c):
        own_w((q,), (c,))
        for dist in range(1, q + 1):
            pass_w(q, dist, c)

    own_w((0, 1, 2), (0,))
    for way in (0, 1):
        there, _ = link(way)

        @pl.when(there)
        def _():
            start_all(zt_copy(z, way))
    for i in range(4):
        start_all(plane_copy(z, i))
    own_w((0,), range(1, CHUNKS))

    def events(k):
        if k == 0:
            pass_w(1, 1, 0)
            pass_w(2, 1, 0)
            tokens(1)
            pass_w(2, 2, 0)
            batch(1, 1)
            relay(0)
        elif k == 1:
            tokens(2)
            batch(1, 2)
            need_w(0)
            own_w((2,), (1,))
        elif k == 2:
            pass_w(2, 1, 1)
            pass_w(2, 2, 1)
            batch(1, 3)
            relay(1)
            tokens(3)
        elif k == 3:
            batch(2, 2)
            batch(1, 4)
            need_w(1)
        elif k == 4:
            batch(2, 3)
            batch(1, 5)
            batch(1, 6)
            relay(2)
        elif k == 5:
            batch(2, 4)
            need_w(2)
        elif k == 6:
            batch(2, 5)
            need_w(3)
        elif k == 7:
            batch(2, 6)
            relay(3)
        else:
            need_w(k - 4)

    def rows_of(s):
        return lax.div(s, per_h), pl.ds(pl.multiple_of(lax.rem(s, per_h) * cap, cap), cap)

    def compact(o, j):
        def one(s, carry):
            meta = meta_all[j, s]
            pos = pick_row(positions(meta, tri_ref[...], cap), e_mine)
            hit = iota_f32((cap, n_tok), 0) == pos
            r_row = (jnp.where(meta[0:1, :] == e_mine, meta[2:3, :], 0.0)
                     + jnp.where(meta[1:2, :] == e_mine, meta[3:4, :], 0.0))
            r_col = jnp.sum(jnp.where(hit, r_row, 0.0), axis=1, keepdims=True)
            got = dot_nn(jnp.where(hit, 1.0, 0.0).astype(BF16), xd_all[j, s])
            h, rows = rows_of(s)
            dy = got[:, d:]
            xc_ref[o * n_h + h, rows, :] = got[:, :d].astype(BF16)
            gc_ref[o * n_h + h, rows, :] = (r_col * dy).astype(BF16)

            @pl.when(o == 0)
            def _():
                dyc_ref[h, rows, :] = dy.astype(BF16)

            return carry

        lax.fori_loop(0, n_p, one, 0)

        def turn(h, carry):
            xt_ref[o * n_h + h] = xc_ref[o * n_h + h, :, own_rows].T
            gt_ref[o * n_h + h] = gc_ref[o * n_h + h, :, own_rows].T
            return carry

        lax.fori_loop(0, n_h, turn, 0)

    def cells(o, c, own):
        cols = pl.ds(pl.multiple_of(c * fc, fc), fc)
        w1, w3, w2 = w_all[0, :, cols], w_all[1, :, cols], w_all[2, :, cols]
        rows = xc_ref.shape[1]
        size = rows // SUB
        subs = [(h, slice(n * size, (n + 1) * size)) for h in range(n_h) for n in range(SUB)]
        sums = [None] * 3
        held = []

        def behind(n):
            h, at = subs[n]
            a, dh1, dh3 = held[n]
            i = o * n_h + h
            for m, (left, right) in enumerate(((xt_ref, dh1), (xt_ref, dh3), (gt_ref, a))):
                term = dot_nn(left[i, :, at], right)
                sums[m] = term if sums[m] is None else sums[m] + term
            if own:
                y_ref[h, at, :] += dot_nt(a, w2)
                dx_ref[h, at, :] += dot_nt(dh1, w1) + dot_nt(dh3, w3)

        for n, (h, at) in enumerate(subs):
            i = o * n_h + h
            h1 = dot_nn(xc_ref[i, at, :], w1)
            h3 = dot_nn(xc_ref[i, at, :], w3)
            da = dot_nn(gc_ref[i, at, :], w2)
            s = jax.nn.sigmoid(h1)
            a = (h1 * s * h3).astype(BF16)
            t = da * s
            dh3 = (t * h1).astype(BF16)
            dh1 = (t * h3 * (1.0 + h1 * (1.0 - s))).astype(BF16)
            held.append((a, dh1, dh3))
            if n:
                behind(n - 1)
        behind(len(subs) - 1)
        for ref, total in zip((dw0_ref, dw1_ref, dwt_ref), sums):
            ref[:, cols] += total

    def send_back():
        def one(s, carry):
            h, rows = rows_of(s)
            dxs_ref[s] = dx_ref[h, rows, :].astype(BF16)
            dr_col = jnp.sum(dyc_ref[h, rows, :].astype(F32) * y_ref[h, rows, :], axis=1, keepdims=True)
            pos = pick_row(positions(meta_all[z, s], tri_ref[...], cap), e_mine)
            hit = iota_f32((cap, n_tok), 0) == pos
            dr_row = jnp.sum(jnp.where(hit, dr_col, 0.0), axis=0, keepdims=True)
            drs_ref[s] = jnp.broadcast_to(dr_row, (8, n_tok))
            return carry

        lax.fori_loop(0, n_p, one, 0)
        for q in range(1, n_p):
            start_all(back_copy(q))
        for c in own_back():
            c.start()

    def back_copy(q):
        to = flip(p, q)
        return (remote(drs_ref.at[to], drr_ref.at[p], s_dr.at[q], r_dr.at[p], {"ep": to}),
                remote(dxs_ref.at[to], dxr_ref.at[p], s_dx.at[q], r_dx.at[p], {"ep": to}))

    def own_back():
        return (pltpu.make_async_copy(dxs_ref.at[p], dxr_ref.at[p], s_dx.at[0]),
                pltpu.make_async_copy(drs_ref.at[p], drr_ref.at[p], s_dr.at[0]))

    n_steps = len(STEPS)

    def step(k, carry):
        for n in range(n_steps):
            @pl.when(k == n)
            def _():
                with jax.named_scope(f"events_{n}"):
                    events(n)

        packed = pick([t[0] for t in STEPS], k)

        @pl.when(packed >= 0)
        def _():
            j = plane_of(packed)
            with jax.named_scope("landed"):
                landed(j)
            with jax.named_scope("compact"):
                compact(packed, j)

        def chunk_own(c, carry):
            with jax.named_scope("cells_own"):
                cells(0, c, True)
            return carry

        lax.fori_loop(pick([t[1][0] for t in STEPS], k), pick([t[1][1] for t in STEPS], k), chunk_own, 0)

        @pl.when(k == n_steps - 1)
        def _():
            with jax.named_scope("send_back"):
                send_back()

        def plane(o, carry):
            def chunk(c, carry):
                with jax.named_scope("cells"):
                    cells(o, c, False)
                return carry

            lo = sum(jnp.where(o == n, pick([t[1 + n][0] for t in STEPS], k), 0) for n in range(1, n_z))
            hi = sum(jnp.where(o == n, pick([t[1 + n][1] for t in STEPS], k), 0) for n in range(1, n_z))
            return lax.fori_loop(lo, hi, chunk, carry)

        return lax.fori_loop(1, n_z, plane, carry)

    lax.fori_loop(0, n_steps, step, 0)

    for c in range(CHUNKS):
        dw2_ref[c * fc:(c + 1) * fc, :] = dwt_ref[:, c * fc:(c + 1) * fc].T
    with jax.named_scope("back_wait"):
        for q in range(1, n_p):
            frm = flip(p, q)
            remote(drs_ref.at[frm], drr_ref.at[frm], s_dr.at[q], r_dr.at[frm], {"ep": frm}).wait_recv()
            remote(dxs_ref.at[frm], dxr_ref.at[frm], s_dx.at[q], r_dx.at[frm], {"ep": frm}).wait_recv()
        for c in own_back():
            c.wait()
    meta = meta_all[z, p]
    pos16 = positions(meta, tri_ref[...], cap)
    gxa_ref[...] = jnp.zeros_like(gxa_ref)
    dr_ref[...] = jnp.zeros_like(dr_ref)

    def gather(e, carry):
        ef = e.astype(F32)
        pos = pick_row(pos16, ef)
        hit = jnp.where(iota_f32((cap, n_tok), 0) == pos, 1.0, 0.0).astype(BF16)
        gxa_ref[...] += dot_tn(hit, dxr_ref[e])
        dr = drr_ref[e]
        dr_ref[...] += jnp.where(meta[0:2, :] == ef, dr[0:1, :], 0.0)
        return carry

    with jax.named_scope("gather"):
        lax.fori_loop(0, n_p, gather, 0)
    gx_ref[...] = gxa_ref[...].astype(BF16)

    with jax.named_scope("drain"):
        for q in range(1, n_p):
            for c in back_copy(q):
                c.wait_send()
        for i in range(4):
            for j in range(n_z):
                for c in plane_copy(j, i):
                    c.wait_send()
        for i in range(3):
            for j in range(n_z):
                for c in relay_copy(j, i):
                    c.wait_send()
        for way in (0, 1):
            there, _ = link(way)
            for dist in range(n_z):
                j = upstream(way, dist)

                @pl.when(valid_z(j) & there)
                def _():
                    for c in zt_copy(j, way):
                        c.wait_send()

                    def drain(c, carry):
                        w_copy(j, c, way).wait_send()
                        return carry

                    lax.fori_loop(0, CHUNKS, drain, 0)


def solution(mesh):
    n_z, n_p = mesh.shape["fsdp"], mesh.shape["ep"]
    tok_spec = P(("fsdp", "ep"), None)
    spec_in = P("ep", "fsdp", None)
    spec_out = P("ep", None, "fsdp")

    def per_device(x_tok, dy_tok, expert_ids, route_w, w_gate, w_up, w_down):
        n_tok, top_k = expert_ids.shape
        d = x_tok.shape[1]
        dl, f = w_gate.shape[1], w_gate.shape[2]
        cap = capacity_of(n_tok, top_k, n_p)
        rows = 4 * cap
        n_t = n_z * n_p // 4
        sem = pltpu.SemaphoreType.DMA
        vmem = pl.BlockSpec(memory_space=pltpu.VMEM)
        hbm = pl.BlockSpec(memory_space=pl.ANY)
        out = jax.ShapeDtypeStruct
        gx, dr, dw0, dw1, dw2 = pl.pallas_call(
            functools.partial(kernel, cap, n_z, n_p),
            out_shape=(out((n_tok, d), BF16), out((top_k, n_tok), F32),
                       out((dl, f), F32), out((dl, f), F32), out((f, dl), F32)),
            in_specs=[vmem] * 2 + [hbm] * 4 + [vmem],
            out_specs=(vmem,) * 5,
            scratch_shapes=[
                pltpu.VMEM((n_z, n_p, n_tok, 2 * d), BF16),
                pltpu.VMEM((n_z, n_p, 8, n_tok), F32),
                pltpu.VMEM((3, n_z * dl, f), BF16),
                pltpu.VMEM((n_tok, n_tok), BF16),
                pltpu.VMEM((n_t, rows, d), BF16),
                pltpu.VMEM((n_t, rows, d), BF16),
                pltpu.VMEM((n_p // 4, rows, d), BF16),
                pltpu.VMEM((n_t, dl, rows), BF16),
                pltpu.VMEM((n_t, dl, rows), BF16),
                pltpu.VMEM((n_p // 4, rows, d), F32),
                pltpu.VMEM((n_p // 4, rows, d), F32),
                pltpu.VMEM((n_p, cap, d), BF16),
                pltpu.VMEM((n_p, cap, d), BF16),
                pltpu.VMEM((n_p, 8, n_tok), F32),
                pltpu.VMEM((n_p, 8, n_tok), F32),
                pltpu.VMEM((n_tok, d), F32),
                pltpu.VMEM((dl, f), F32),
                sem((2, n_z)), sem((n_z,)), sem((2, n_z)), sem((n_z,)),
                sem((2, n_z, CHUNKS)), sem((n_z, CHUNKS)),
                sem((n_z, 4)), sem((n_z, n_p)), sem((n_z, 4)), sem((n_z, n_p)),
                sem((n_z, 3)), sem((n_z, 3)),
                sem((n_p,)), sem((n_p,)), sem((n_p,)), sem((n_p,)),
                sem((4,)),
            ],
            compiler_params=pltpu.CompilerParams(
                collective_id=0, has_side_effects=True, vmem_limit_bytes=67043328),
        )(expert_ids.T, route_w.T, x_tok, dy_tok, w_gate, w_up, w_down)
        return gx, dr.T, dw0[None], dw1[None], dw2[None]

    return jax.shard_map(
        per_device, mesh=mesh,
        in_specs=(tok_spec, tok_spec, tok_spec, tok_spec, spec_in, spec_in, spec_out),
        out_specs=(tok_spec, tok_spec, spec_in, spec_in, spec_out),
        check_vma=False)
```

time: 219 us -> 174 us (0.79)
  the two profiles are of different devices: /device:TPU:25 before, /device:TPU:0 now
where the time goes in v2:
time: 174 us; the launch traced here: 173 us
  Pallas kernels  165 us (95%)
  local copies, waits for them, and re-layouts  6.93 us (4%)
    pallas_call x1, Pallas kernels, per_device(): pl.pallas_call(functools.partial(kernel, cap, n_z, n_p), out_shape=(out((...  165 us
    unnamed x11, local copies, waits for them, and re-layouts  6.93 us

profile of v2, /device:TPU:0, one launch (start us, length us, event | category | flops | bytes accessed | tf_op | source)
XLA Modules:
  0.0 172.8 jit_solution(4923838090868643758)
XLA Ops:
  0.6 165.2 %shard_map.110 = (bf16[256,512]{1,0:T(8,128)(2,1)}, f32[2,256]{1,0:T(2,128)}, f32[128,1792]{1,0:T(8,128)}, f32[128,1792]{1,0:T(8,128)}, f32[1792,128]{1,0:T(8,128)}) custom-call(s32[2,256]{1,0:T(2,128)} %bitcast.10, f32[2,256]{1,0:T(2,128)} %bitcast.11, bf16[256,512]{1,0:T(8,128)(2,1)} %x_ref.1, bf16[256,512]{1,0:T(8,128)(2,1)} %dy_ref.1, ...), custom_call_target="tpu_custom_call" | custom-call | tf_op jit(solution)/shard_map/pallas_call | solution.py:501
  165.8 0.0 copy-start.2
  165.9 1.7 copy.17
  167.5 0.0 copy-done.2
  167.5 0.6 copy.18
  168.1 0.0 copy-start.1
  168.1 2.2 %copy.19 = f32[1,128,1792]{2,1,0:T(8,128)} copy(f32[1,128,1792]{2,1,0:T(8,128)} %bitcast.8) | data formatting | bytes 1835008
  170.3 0.0 copy-done.1
  170.3 0.0 copy-start
  170.4 0.9 copy.20
  171.3 0.6 copy-done
  171.9 0.9 copy.21
Async XLA Ops:
  165.8 1.7 copy-start.2
  168.1 2.2 %copy-start.1 = (f32[128,1792]{1,0:T(8,128)S(1)}, f32[128,1792]{1,0:T(8,128)}, u32[]{:S(2)}) copy-start(f32[128,1792]{1,0:T(8,128)} %get-tuple-element.13) | copy-start | bytes 2752516
  170.3 1.5 copy-start

commit v3 on v2

--- a/solution.py
+++ b/solution.py
@@ -15,6 +15,7 @@
 DIAG = (2, 4, 6)
 DIRECT = (1, 2, 4, 6)
 SUB = 3
+RETURN = (6, 4, 7, 5, 2, 3, 1, 0)
 ORDER = ((0, 1, 2, 3), (1, 0, 2, 3), (2, 1, 3, 0), (3, 2, 1, 0))
 STEPS = (
     (0, (0, 0), (0, 0), (0, 0), (0, 0)),
@@ -25,9 +26,9 @@
     (-1, (2, 3), (2, 3), (2, 3), (0, 0)),
     (-1, (3, 4), (3, 4), (3, 4), (0, 0)),
     (3, (0, 0), (0, 0), (0, 0), (0, 4)),
-    (-1, (4, 5), (4, 5), (4, 5), (4, 5)),
-    (-1, (5, 6), (5, 6), (5, 6), (5, 6)),
-    (-1, (6, 7), (6, 7), (6, 7), (6, 7)),
+    (-1, (4, 5), (0, 0), (0, 0), (0, 0)),
+    (-1, (5, 6), (4, 5), (4, 5), (4, 5)),
+    (-1, (6, 7), (5, 7), (5, 7), (5, 7)),
 )
 
 
@@ -37,8 +38,11 @@
 
 def flip(p, q):
     for b in (1, 2, 4):
-        if q & b:
-            p = p + b - 2 * b * lax.rem(lax.div(p, b), 2)
+        turned = b - 2 * b * lax.rem(lax.div(p, b), 2)
+        if isinstance(q, int):
+            p = p + turned if q & b else p
+        else:
+            p = p + lax.rem(lax.div(q, b), 2) * turned
     return p
 
 
@@ -56,6 +60,10 @@
 
 def iota_f32(shape, dim):
     return lax.broadcasted_iota(jnp.int32, shape, dim).astype(F32)
+
+
+def earlier(n):
+    return jnp.where(iota_f32((n, n), 0) < iota_f32((n, n), 1), 1.0, 0.0).astype(BF16)
 
 
 def positions(meta, tri, cap):
@@ -76,9 +84,9 @@
 
 
 def kernel(cap, n_z, n_p, ids_ref, rw_ref, x_ref, dy_ref, wg_ref, wu_ref, wd_ref,
-           gx_ref, dr_ref, dw0_ref, dw1_ref, dw2_ref,
-           xd_all, meta_all, w_all, tri_ref, xc_ref, gc_ref, dyc_ref, xt_ref, gt_ref, y_ref, dx_ref,
-           dxs_ref, dxr_ref, drs_ref, drr_ref, gxa_ref, dwt_ref,
+           dxr_ref, drr_ref, dw0_out, dw1_out, dw2_out,
+           xd_all, meta_all, w_all, tri_ref, xc_ref, gc_ref, dyc_ref, xt_ref, gt_ref, dy_y_ref, dx_ref,
+           dxs_ref, drs_ref, dw0_ref, dw1_ref, dwt_ref, dw2_ref, wd_own,
            s_zt, r_zt, s_zm, r_zm, s_w, r_w, s_p, r_p, s_pm, r_pm, s_r, s_rm,
            s_dx, r_dx, s_dr, r_dr, s_loc):
     z = lax.axis_index("fsdp")
@@ -97,15 +105,6 @@
             return pick([t[o] for t in ORDER], z)
         return sum(jnp.where(z == n, pick(t, o), 0) for n, t in enumerate(ORDER))
 
-    loads = (
-        pltpu.make_async_copy(x_ref, xd_all.at[z, p, :, pl.ds(0, d)], s_loc.at[0]),
-        pltpu.make_async_copy(dy_ref, xd_all.at[z, p, :, pl.ds(d, d)], s_loc.at[1]),
-        pltpu.make_async_copy(wg_ref.at[0], w_all.at[0, own_rows, :], s_loc.at[2]),
-        pltpu.make_async_copy(wu_ref.at[0], w_all.at[1, own_rows, :], s_loc.at[3]),
-    )
-    for c in loads:
-        c.start()
-
     barrier = pltpu.get_barrier_semaphore()
     for q in range(1, n_p):
         pl.semaphore_signal(barrier, inc=1, device_id={"ep": flip(p, q)}, device_id_type=MESH)
@@ -116,14 +115,22 @@
         def _():
             pl.semaphore_signal(barrier, inc=1, device_id={"fsdp": nb}, device_id_type=MESH)
 
-    for c in range(CHUNKS):
-        w_all[2, own_rows, c * fc:(c + 1) * fc] = wd_ref[0, c * fc:(c + 1) * fc, :].T
+    load_wd = pltpu.make_async_copy(wd_ref.at[0], wd_own, s_loc.at[4])
+    loads = (
+        pltpu.make_async_copy(wg_ref.at[0], w_all.at[0, own_rows, :], s_loc.at[2]),
+        pltpu.make_async_copy(wu_ref.at[0], w_all.at[1, own_rows, :], s_loc.at[3]),
+        pltpu.make_async_copy(x_ref, xd_all.at[z, p, :, pl.ds(0, d)], s_loc.at[0]),
+        pltpu.make_async_copy(dy_ref, xd_all.at[z, p, :, pl.ds(d, d)], s_loc.at[1]),
+    )
+    load_wd.start()
+    for c in loads:
+        c.start()
     meta_all[z, p, 0:2, :] = ids_ref[...].astype(F32)
     meta_all[z, p, 2:4, :] = rw_ref[...]
     meta_all[z, p, 4:8, :] = jnp.zeros((4, n_tok), F32)
-    tri_ref[...] = jnp.where(iota_f32((n_tok, n_tok), 0) < iota_f32((n_tok, n_tok), 1), 1.0, 0.0).astype(BF16)
-    for ref in (dw0_ref, dw1_ref, dwt_ref, y_ref, dx_ref):
-        ref[...] = jnp.zeros_like(ref)
+    load_wd.wait()
+    for c in range(CHUNKS):
+        w_all[2, own_rows, c * fc:(c + 1) * fc] = wd_own[c * fc:(c + 1) * fc, :].T
     for c in loads:
         c.wait()
     inner = jnp.where(z > 0, 1, 0) + jnp.where(z < n_z - 1, 1, 0)
@@ -244,6 +251,9 @@
     for i in range(4):
         start_all(plane_copy(z, i))
     own_w((0,), range(1, CHUNKS))
+    tri_ref[...] = earlier(n_tok)
+    for ref in (dw0_ref, dw1_ref, dwt_ref, dy_y_ref, dx_ref):
+        ref[...] = jnp.zeros_like(ref)
 
     def events(k):
         if k == 0:
@@ -334,7 +344,9 @@
                 term = dot_nn(left[i, :, at], right)
                 sums[m] = term if sums[m] is None else sums[m] + term
             if own:
-                y_ref[h, at, :] += dot_nt(a, w2)
+                grown = dyc_ref[h, at, :].astype(F32) * dot_nt(a, w2)
+                wide = dy_y_ref.shape[2]
+                dy_y_ref[h, at, :] += sum(grown[:, m:m + wide] for m in range(0, d, wide))
                 dx_ref[h, at, :] += dot_nt(dh1, w1) + dot_nt(dh3, w3)
 
         for n, (h, at) in enumerate(subs):
@@ -355,30 +367,43 @@
             ref[:, cols] += total
 
     def send_back():
-        def one(s, carry):
+        def leave(n):
+            to = flip(p, pick(RETURN, n))
+
+            @pl.when(to != p)
+            def _():
+                start_all(back_copy(to))
+
+            @pl.when(to == p)
+            def _():
+                start_all(own_back())
+
+        def one(n, carry):
+            s = flip(p, pick(RETURN, n))
             h, rows = rows_of(s)
             dxs_ref[s] = dx_ref[h, rows, :].astype(BF16)
-            dr_col = jnp.sum(dyc_ref[h, rows, :].astype(F32) * y_ref[h, rows, :], axis=1, keepdims=True)
+            dr_col = jnp.sum(dy_y_ref[h, rows, :], axis=1, keepdims=True)
             pos = pick_row(positions(meta_all[z, s], tri_ref[...], cap), e_mine)
             hit = iota_f32((cap, n_tok), 0) == pos
             dr_row = jnp.sum(jnp.where(hit, dr_col, 0.0), axis=0, keepdims=True)
             drs_ref[s] = jnp.broadcast_to(dr_row, (8, n_tok))
+
+            @pl.when(n > 0)
+            def _():
+                leave(n - 1)
+
             return carry
 
         lax.fori_loop(0, n_p, one, 0)
-        for q in range(1, n_p):
-            start_all(back_copy(q))
-        for c in own_back():
-            c.start()
-
-    def back_copy(q):
-        to = flip(p, q)
-        return (remote(drs_ref.at[to], drr_ref.at[p], s_dr.at[q], r_dr.at[p], {"ep": to}),
-                remote(dxs_ref.at[to], dxr_ref.at[p], s_dx.at[q], r_dx.at[p], {"ep": to}))
+        leave(n_p - 1)
+
+    def back_copy(to):
+        return (remote(drs_ref.at[to], drr_ref.at[p], s_dr.at[to], r_dr.at[p], {"ep": to}),
+                remote(dxs_ref.at[to], dxr_ref.at[p], s_dx.at[to], r_dx.at[p], {"ep": to}))
 
     def own_back():
-        return (pltpu.make_async_copy(dxs_ref.at[p], dxr_ref.at[p], s_dx.at[0]),
-                pltpu.make_async_copy(drs_ref.at[p], drr_ref.at[p], s_dr.at[0]))
+        return (pltpu.make_async_copy(drs_ref.at[p], drr_ref.at[p], s_dr.at[p]),
+                pltpu.make_async_copy(dxs_ref.at[p], dxr_ref.at[p], s_dx.at[p]))
 
     n_steps = len(STEPS)
 
@@ -425,36 +450,26 @@
 
     lax.fori_loop(0, n_steps, step, 0)
 
+    stores = [pltpu.make_async_copy(dw0_ref, dw0_out, s_loc.at[0]),
+              pltpu.make_async_copy(dw1_ref, dw1_out, s_loc.at[1]),
+              pltpu.make_async_copy(dw2_ref, dw2_out, s_loc.at[2])]
     for c in range(CHUNKS):
         dw2_ref[c * fc:(c + 1) * fc, :] = dwt_ref[:, c * fc:(c + 1) * fc].T
+    for c in stores:
+        c.start()
     with jax.named_scope("back_wait"):
         for q in range(1, n_p):
             frm = flip(p, q)
-            remote(drs_ref.at[frm], drr_ref.at[frm], s_dr.at[q], r_dr.at[frm], {"ep": frm}).wait_recv()
-            remote(dxs_ref.at[frm], dxr_ref.at[frm], s_dx.at[q], r_dx.at[frm], {"ep": frm}).wait_recv()
+            remote(drs_ref.at[frm], drr_ref.at[frm], s_dr.at[frm], r_dr.at[frm], {"ep": frm}).wait_recv()
+            remote(dxs_ref.at[frm], dxr_ref.at[frm], s_dx.at[frm], r_dx.at[frm], {"ep": frm}).wait_recv()
         for c in own_back():
             c.wait()
-    meta = meta_all[z, p]
-    pos16 = positions(meta, tri_ref[...], cap)
-    gxa_ref[...] = jnp.zeros_like(gxa_ref)
-    dr_ref[...] = jnp.zeros_like(dr_ref)
-
-    def gather(e, carry):
-        ef = e.astype(F32)
-        pos = pick_row(pos16, ef)
-        hit = jnp.where(iota_f32((cap, n_tok), 0) == pos, 1.0, 0.0).astype(BF16)
-        gxa_ref[...] += dot_tn(hit, dxr_ref[e])
-        dr = drr_ref[e]
-        dr_ref[...] += jnp.where(meta[0:2, :] == ef, dr[0:1, :], 0.0)
-        return carry
-
-    with jax.named_scope("gather"):
-        lax.fori_loop(0, n_p, gather, 0)
-    gx_ref[...] = gxa_ref[...].astype(BF16)
+    for c in stores:
+        c.wait()
 
     with jax.named_scope("drain"):
         for q in range(1, n_p):
-            for c in back_copy(q):
+            for c in back_copy(flip(p, q)):
                 c.wait_send()
         for i in range(4):
             for j in range(n_z):
@@ -481,6 +496,45 @@
                     lax.fori_loop(0, CHUNKS, drain, 0)
 
 
+def finish(cap, n_p, ids_ref, dxr_hbm, drr_hbm, dw0_in, dw1_in, dw2_in,
+           gx_ref, dr_ref, dw0_out, dw1_out, dw2_out,
+           dxr_ref, drr_ref, dw0_ref, dw1_ref, dw2_ref, gxa_ref, s_in, s_out):
+    n_tok = ids_ref.shape[1]
+    rows_in = (pltpu.make_async_copy(dxr_hbm, dxr_ref, s_in.at[0]),
+               pltpu.make_async_copy(drr_hbm, drr_ref, s_in.at[1]))
+    moves = tuple(
+        (pltpu.make_async_copy(src, mid, s_in.at[2 + n]), pltpu.make_async_copy(mid, dst, s_out.at[n]))
+        for n, (src, mid, dst) in enumerate(
+            ((dw0_in, dw0_ref, dw0_out), (dw1_in, dw1_ref, dw1_out), (dw2_in, dw2_ref, dw2_out))))
+    for c in rows_in:
+        c.start()
+    for c, _ in moves:
+        c.start()
+    ids = ids_ref[...].astype(F32)
+    pos16 = positions(ids, earlier(n_tok), cap)
+    gxa_ref[...] = jnp.zeros_like(gxa_ref)
+    dr_ref[...] = jnp.zeros_like(dr_ref)
+    for c in rows_in:
+        c.wait()
+    for c_in, c_out in moves:
+        c_in.wait()
+        c_out.start()
+
+    def gather(e, carry):
+        ef = e.astype(F32)
+        pos = pick_row(pos16, ef)
+        hit = jnp.where(iota_f32((cap, n_tok), 0) == pos, 1.0, 0.0).astype(BF16)
+        gxa_ref[...] += dot_tn(hit, dxr_ref[e])
+        dr = drr_ref[e]
+        dr_ref[...] += jnp.where(ids == ef, dr[0:1, :], 0.0)
+        return carry
+
+    lax.fori_loop(0, n_p, gather, 0)
+    gx_ref[...] = gxa_ref[...].astype(BF16)
+    for _, c in moves:
+        c.wait()
+
+
 def solution(mesh):
     n_z, n_p = mesh.shape["fsdp"], mesh.shape["ep"]
     tok_spec = P(("fsdp", "ep"), None)
@@ -498,12 +552,13 @@
         vmem = pl.BlockSpec(memory_space=pltpu.VMEM)
         hbm = pl.BlockSpec(memory_space=pl.ANY)
         out = jax.ShapeDtypeStruct
-        gx, dr, dw0, dw1, dw2 = pl.pallas_call(
+        ids, rw = expert_ids.T, route_w.T
+        dw_shapes = (out((dl, f), F32), out((dl, f), F32), out((f, dl), F32))
+        back = pl.pallas_call(
             functools.partial(kernel, cap, n_z, n_p),
-            out_shape=(out((n_tok, d), BF16), out((top_k, n_tok), F32),
-                       out((dl, f), F32), out((dl, f), F32), out((f, dl), F32)),
-            in_specs=[vmem] * 2 + [hbm] * 4 + [vmem],
-            out_specs=(vmem,) * 5,
+            out_shape=(out((n_p, cap, d), BF16), out((n_p, 8, n_tok), F32)) + dw_shapes,
+            in_specs=[vmem] * 2 + [hbm] * 5,
+            out_specs=(hbm,) * 5,
             scratch_shapes=[
                 pltpu.VMEM((n_z, n_p, n_tok, 2 * d), BF16),
                 pltpu.VMEM((n_z, n_p, 8, n_tok), F32),
@@ -514,24 +569,40 @@
                 pltpu.VMEM((n_p // 4, rows, d), BF16),
                 pltpu.VMEM((n_t, dl, rows), BF16),
                 pltpu.VMEM((n_t, dl, rows), BF16),
-                pltpu.VMEM((n_p // 4, rows, d), F32),
+                pltpu.VMEM((n_p // 4, rows, min(128, d)), F32),
                 pltpu.VMEM((n_p // 4, rows, d), F32),
                 pltpu.VMEM((n_p, cap, d), BF16),
-                pltpu.VMEM((n_p, cap, d), BF16),
                 pltpu.VMEM((n_p, 8, n_tok), F32),
-                pltpu.VMEM((n_p, 8, n_tok), F32),
-                pltpu.VMEM((n_tok, d), F32),
                 pltpu.VMEM((dl, f), F32),
+                pltpu.VMEM((dl, f), F32),
+                pltpu.VMEM((dl, f), F32),
+                pltpu.VMEM((f, dl), F32),
+                pltpu.VMEM((f, dl), BF16),
                 sem((2, n_z)), sem((n_z,)), sem((2, n_z)), sem((n_z,)),
                 sem((2, n_z, CHUNKS)), sem((n_z, CHUNKS)),
                 sem((n_z, 4)), sem((n_z, n_p)), sem((n_z, 4)), sem((n_z, n_p)),
                 sem((n_z, 3)), sem((n_z, 3)),
                 sem((n_p,)), sem((n_p,)), sem((n_p,)), sem((n_p,)),
-                sem((4,)),
+                sem((5,)),
             ],
             compiler_params=pltpu.CompilerParams(
                 collective_id=0, has_side_effects=True, vmem_limit_bytes=67043328),
-        )(expert_ids.T, route_w.T, x_tok, dy_tok, w_gate, w_up, w_down)
+        )(ids, rw, x_tok, dy_tok, w_gate, w_up, w_down)
+        gx, dr, dw0, dw1, dw2 = pl.pallas_call(
+            functools.partial(finish, cap, n_p),
+            out_shape=(out((n_tok, d), BF16), out((top_k, n_tok), F32)) + dw_shapes,
+            in_specs=[vmem] + [hbm] * 5,
+            out_specs=(vmem,) * 2 + (hbm,) * 3,
+            scratch_shapes=[
+                pltpu.VMEM((n_p, cap, d), BF16),
+                pltpu.VMEM((n_p, 8, n_tok), F32),
+                pltpu.VMEM((dl, f), F32),
+                pltpu.VMEM((dl, f), F32),
+                pltpu.VMEM((f, dl), F32),
+                pltpu.VMEM((n_tok, d), F32),
+                sem((5,)), sem((3,)),
+            ],
+        )(ids, *back)
         return gx, dr.T, dw0[None], dw1[None], dw2[None]
 
     return jax.shard_map(

time: 174 us -> 161 us (0.925)
  local copies, waits for them, and re-layouts: 6.93 us -> 0 us
  Pallas kernels: 165 us -> 161 us
    pallas_call x1, Pallas kernels: 165 us -> 155 us  [per_device(): pl.pallas_call(functools.partial(kernel, cap, n_z, n_p), out_shape=(out((...]
    unnamed x11 -> x0, local copies, waits for them, and re-layouts: 6.93 us -> none
    pallas_call x0 -> x1, Pallas kernels: none -> 5.8 us  [per_device(): pl.pallas_call(functools.partial(finish, cap, n_p), out_shape=(out((n_tok...]
where the time goes in v3:
time: 161 us
  Pallas kernels  161 us (100%)
    pallas_call x1, Pallas kernels, per_device(): pl.pallas_call(functools.partial(kernel, cap, n_z, n_p), out_shape=(out((...  155 us
    pallas_call x1, Pallas kernels, per_device(): pl.pallas_call(functools.partial(finish, cap, n_p), out_shape=(out((n_tok...  5.8 us

profile of v3, /device:TPU:0, one launch (start us, length us, event | category | flops | bytes accessed | tf_op | source)
XLA Modules:
  0.0 161.2 jit_solution(6447044467115339160)
XLA Ops:
  0.6 154.8 %shard_map.110 = (bf16[8,192,512]{2,1,0:T(8,128)(2,1)}, f32[8,8,256]{2,1,0:T(8,128)}, f32[128,1792]{1,0:T(8,128)}, f32[128,1792]{1,0:T(8,128)}, f32[1792,128]{1,0:T(8,128)}) custom-call(s32[2,256]{1,0:T(2,128)} %bitcast.6, f32[2,256]{1,0:T(2,128)} %bitcast.8, bf16[256,512]{1,0:T(8,128)(2,1)} %x_ref.1, bf16[256,512]{1,0:T(8,128)(2,1)} %dy_ref.1, ...), custom_call_target="tpu_custom_call" | custom-call | tf_op jit(solution)/shard_map/pallas_call | solution.py:557
  155.4 5.8 %shard_map.111 = (bf16[256,512]{1,0:T(8,128)(2,1)}, f32[2,256]{1,0:T(2,128)}, f32[128,1792]{1,0:T(8,128)}, f32[128,1792]{1,0:T(8,128)}, f32[1792,128]{1,0:T(8,128)}) custom-call(s32[2,256]{1,0:T(2,128)} %bitcast.7, bf16[8,192,512]{2,1,0:T(8,128)(2,1)} %get-tuple-element.15.dxr_hbm, f32[8,8,256]{2,1,0:T(8,128)} %get-tuple-element.16.drr_hbm, ...), custom_call_target="tpu_custom_call" | custom-call | tf_op jit(solution)/shard_map/pallas_call | solution.py:591

commit v4 on v3

--- a/solution.py
+++ b/solution.py
@@ -16,20 +16,36 @@
 DIRECT = (1, 2, 4, 6)
 SUB = 3
 RETURN = (6, 4, 7, 5, 2, 3, 1, 0)
-ORDER = ((0, 1, 2, 3), (1, 0, 2, 3), (2, 1, 3, 0), (3, 2, 1, 0))
-STEPS = (
-    (0, (0, 0), (0, 0), (0, 0), (0, 0)),
-    (-1, (0, 1), (0, 0), (0, 0), (0, 0)),
-    (1, (0, 0), (0, 1), (0, 0), (0, 0)),
-    (-1, (1, 2), (1, 2), (0, 0), (0, 0)),
-    (2, (0, 0), (0, 0), (0, 2), (0, 0)),
-    (-1, (2, 3), (2, 3), (2, 3), (0, 0)),
-    (-1, (3, 4), (3, 4), (3, 4), (0, 0)),
-    (3, (0, 0), (0, 0), (0, 0), (0, 4)),
-    (-1, (4, 5), (0, 0), (0, 0), (0, 0)),
-    (-1, (5, 6), (4, 5), (4, 5), (4, 5)),
-    (-1, (6, 7), (5, 7), (5, 7), (5, 7)),
+ORDER = ((0, 1, 2, 3), (1, 0, 2, 3), (2, 3, 1, 0), (3, 2, 1, 0))
+NONE = (0, 0)
+END_STEPS = (
+    (0, NONE, NONE, NONE, NONE),
+    (-1, (0, 1), NONE, NONE, NONE),
+    (1, NONE, (0, 1), NONE, NONE),
+    (-1, (1, 2), (1, 2), NONE, NONE),
+    (2, NONE, NONE, (0, 2), NONE),
+    (-1, (2, 3), (2, 3), (2, 3), NONE),
+    (-1, (3, 4), (3, 4), (3, 4), NONE),
+    (3, NONE, NONE, NONE, (0, 4)),
+    (-1, (4, 5), (4, 5), (4, 5), (4, 5)),
+    (-1, (5, 6), (5, 6), (5, 6), (5, 6)),
+    (-1, (6, 7), (6, 7), (6, 7), (6, 7)),
 )
+MID_STEPS = (
+    (0, (0, 1), NONE, NONE, NONE),
+    (-1, (1, 2), NONE, NONE, NONE),
+    (1, (2, 3), (0, 1), NONE, NONE),
+    (-1, (3, 4), (1, 4), NONE, NONE),
+    (-1, (4, 5), (4, 5), NONE, NONE),
+    (-1, (5, 6), (5, 6), NONE, NONE),
+    (-1, (6, 7), (6, 7), NONE, NONE),
+    (2, NONE, NONE, (0, 7), NONE),
+    (3, NONE, NONE, NONE, NONE),
+    (-1, NONE, NONE, NONE, (0, 7)),
+    (-1, NONE, NONE, NONE, NONE),
+)
+SEND_STEP = 6
+GATHER_STEP = 9
 
 
 def capacity_of(tok_dev, top_k, experts):
@@ -84,11 +100,12 @@
 
 
 def kernel(cap, n_z, n_p, ids_ref, rw_ref, x_ref, dy_ref, wg_ref, wu_ref, wd_ref,
-           dxr_ref, drr_ref, dw0_out, dw1_out, dw2_out,
+           gx_out, dr_out, dw0_out, dw1_out, dw2_out,
            xd_all, meta_all, w_all, tri_ref, xc_ref, gc_ref, dyc_ref, xt_ref, gt_ref, dy_y_ref, dx_ref,
-           dxs_ref, drs_ref, dw0_ref, dw1_ref, dwt_ref, dw2_ref, wd_own,
+           dxs_ref, drs_ref, dxr_ref, drr_ref, gxa_ref, gx_ref, dr_ref,
+           dw0_ref, dw1_ref, dwt_ref, dw2_ref, wd_own,
            s_zt, r_zt, s_zm, r_zm, s_w, r_w, s_p, r_p, s_pm, r_pm, s_r, s_rm,
-           s_dx, r_dx, s_dr, r_dr, s_loc):
+           s_dx, r_dx, s_dr, r_dr, s_gx, r_gx, s_loc):
     z = lax.axis_index("fsdp")
     p = lax.axis_index("ep")
     e_mine = p.astype(F32)
@@ -98,6 +115,7 @@
     per_h = 4
     n_h = n_p // per_h
     partner = flip(p, 1)
+    mid = (z > 0) & (z < n_z - 1)
     own_rows = pl.ds(pl.multiple_of(z * dl, dl), dl)
 
     def plane_of(o):
@@ -209,11 +227,11 @@
                     w_copy(j, c, way).wait_recv()
 
     def tokens(dist):
-        for way in (0, 1):
+        for way, turn in ((0, z < 2), (1, z >= 0), (0, z >= 2)):
             there, _ = link(way)
             j = upstream(way, dist)
 
-            @pl.when(valid_z(j))
+            @pl.when(turn & valid_z(j))
             def _():
                 for c in zt_copy(j, way):
                     c.wait_recv()
@@ -255,7 +273,28 @@
     for ref in (dw0_ref, dw1_ref, dwt_ref, dy_y_ref, dx_ref):
         ref[...] = jnp.zeros_like(ref)
 
-    def events(k):
+    def end_events(k):
+        if k == 0:
+            tokens(1)
+            relay(0)
+        elif k == 1:
+            tokens(2)
+            need_w(0)
+        elif k == 2:
+            relay(1)
+            tokens(3)
+        elif k == 3:
+            need_w(1)
+        elif k == 4:
+            relay(2)
+        elif k in (5, 6):
+            need_w(k - 3)
+        elif k == 7:
+            relay(3)
+        else:
+            need_w(k - 4)
+
+    def mid_events(k):
         if k == 0:
             pass_w(1, 1, 0)
             pass_w(2, 1, 0)
@@ -266,39 +305,28 @@
         elif k == 1:
             tokens(2)
             batch(1, 2)
-            need_w(0)
-            own_w((2,), (1,))
+            batch(2, 1)
         elif k == 2:
-            pass_w(2, 1, 1)
-            pass_w(2, 2, 1)
             batch(1, 3)
             relay(1)
-            tokens(3)
+            batch(2, 2)
         elif k == 3:
-            batch(2, 2)
+            batch(2, 3)
             batch(1, 4)
-            need_w(1)
-        elif k == 4:
-            batch(2, 3)
             batch(1, 5)
             batch(1, 6)
+        elif k == 4:
             relay(2)
-        elif k == 5:
             batch(2, 4)
-            need_w(2)
-        elif k == 6:
-            batch(2, 5)
-            need_w(3)
+        elif k in (5, 6):
+            batch(2, k)
         elif k == 7:
-            batch(2, 6)
             relay(3)
-        else:
-            need_w(k - 4)
 
     def rows_of(s):
         return lax.div(s, per_h), pl.ds(pl.multiple_of(lax.rem(s, per_h) * cap, cap), cap)
 
-    def compact(o, j):
+    def compact(o, j, keep_dy):
         def one(s, carry):
             meta = meta_all[j, s]
             pos = pick_row(positions(meta, tri_ref[...], cap), e_mine)
@@ -312,13 +340,11 @@
             xc_ref[o * n_h + h, rows, :] = got[:, :d].astype(BF16)
             gc_ref[o * n_h + h, rows, :] = (r_col * dy).astype(BF16)
 
-            @pl.when(o == 0)
-            def _():
-                dyc_ref[h, rows, :] = dy.astype(BF16)
-
+            if keep_dy:
+                dyc_ref[o, h, rows, :] = dy.astype(BF16)
             return carry
 
-        lax.fori_loop(0, n_p, one, 0)
+        lax.fori_loop(0, n_p, one, 0, unroll=2)
 
         def turn(h, carry):
             xt_ref[o * n_h + h] = xc_ref[o * n_h + h, :, own_rows].T
@@ -344,10 +370,10 @@
                 term = dot_nn(left[i, :, at], right)
                 sums[m] = term if sums[m] is None else sums[m] + term
             if own:
-                grown = dyc_ref[h, at, :].astype(F32) * dot_nt(a, w2)
-                wide = dy_y_ref.shape[2]
-                dy_y_ref[h, at, :] += sum(grown[:, m:m + wide] for m in range(0, d, wide))
-                dx_ref[h, at, :] += dot_nt(dh1, w1) + dot_nt(dh3, w3)
+                grown = dyc_ref[o, h, at, :].astype(F32) * dot_nt(a, w2)
+                wide = dy_y_ref.shape[-1]
+                dy_y_ref[o, h, at, :] += sum(grown[:, m:m + wide] for m in range(0, d, wide))
+                dx_ref[o, h, at, :] += dot_nt(dh1, w1) + dot_nt(dh3, w3)
 
         for n, (h, at) in enumerate(subs):
             i = o * n_h + h
@@ -366,27 +392,29 @@
         for ref, total in zip((dw0_ref, dw1_ref, dwt_ref), sums):
             ref[:, cols] += total
 
-    def send_back():
+    def send_back(o):
+        j = plane_of(o)
+
         def leave(n):
             to = flip(p, pick(RETURN, n))
 
             @pl.when(to != p)
             def _():
-                start_all(back_copy(to))
+                start_all(back_copy(o, to))
 
             @pl.when(to == p)
             def _():
-                start_all(own_back())
+                start_all(own_back(o))
 
         def one(n, carry):
             s = flip(p, pick(RETURN, n))
             h, rows = rows_of(s)
-            dxs_ref[s] = dx_ref[h, rows, :].astype(BF16)
-            dr_col = jnp.sum(dy_y_ref[h, rows, :], axis=1, keepdims=True)
-            pos = pick_row(positions(meta_all[z, s], tri_ref[...], cap), e_mine)
+            dxs_ref[o, s] = dx_ref[o, h, rows, :].astype(BF16)
+            dr_col = jnp.sum(dy_y_ref[o, h, rows, :], axis=1, keepdims=True)
+            pos = pick_row(positions(meta_all[j, s], tri_ref[...], cap), e_mine)
             hit = iota_f32((cap, n_tok), 0) == pos
             dr_row = jnp.sum(jnp.where(hit, dr_col, 0.0), axis=0, keepdims=True)
-            drs_ref[s] = jnp.broadcast_to(dr_row, (8, n_tok))
+            drs_ref[o, s] = jnp.broadcast_to(dr_row, (8, n_tok))
 
             @pl.when(n > 0)
             def _():
@@ -397,44 +425,113 @@
         lax.fori_loop(0, n_p, one, 0)
         leave(n_p - 1)
 
-    def back_copy(to):
-        return (remote(drs_ref.at[to], drr_ref.at[p], s_dr.at[to], r_dr.at[p], {"ep": to}),
-                remote(dxs_ref.at[to], dxr_ref.at[p], s_dx.at[to], r_dx.at[p], {"ep": to}))
-
-    def own_back():
-        return (pltpu.make_async_copy(drs_ref.at[p], drr_ref.at[p], s_dr.at[p]),
-                pltpu.make_async_copy(dxs_ref.at[p], dxr_ref.at[p], s_dx.at[p]))
-
-    n_steps = len(STEPS)
+    def back_copy(o, to):
+        return (remote(drs_ref.at[o, to], drr_ref.at[o, p], s_dr.at[o, to], r_dr.at[o, p], {"ep": to}),
+                remote(dxs_ref.at[o, to], dxr_ref.at[o, p], s_dx.at[o, to], r_dx.at[o, p], {"ep": to}))
+
+    def own_back(o):
+        return (pltpu.make_async_copy(drs_ref.at[o, p], drr_ref.at[o, p], s_dr.at[o, p]),
+                pltpu.make_async_copy(dxs_ref.at[o, p], dxr_ref.at[o, p], s_dx.at[o, p]))
+
+    def gather(o):
+        meta = meta_all[plane_of(o), p]
+        pos16 = positions(meta, tri_ref[...], cap)
+        gxa_ref[...] = jnp.zeros_like(gxa_ref)
+        dr_ref[o] = jnp.zeros_like(dr_ref[o])
+
+        def one(n, carry):
+            e = flip(p, pick(RETURN, n))
+
+            @pl.when(e != p)
+            def _():
+                remote(drs_ref.at[o, e], drr_ref.at[o, e], s_dr.at[o, e], r_dr.at[o, e], {"ep": e}).wait_recv()
+                remote(dxs_ref.at[o, e], dxr_ref.at[o, e], s_dx.at[o, e], r_dx.at[o, e], {"ep": e}).wait_recv()
+
+            @pl.when(e == p)
+            def _():
+                for c in own_back(o):
+                    c.wait()
+
+            ef = e.astype(F32)
+            pos = pick_row(pos16, ef)
+            hit = jnp.where(iota_f32((cap, n_tok), 0) == pos, 1.0, 0.0).astype(BF16)
+            gxa_ref[...] += dot_tn(hit, dxr_ref[o, e])
+            dr = drr_ref[o, e]
+            dr_ref[o] += jnp.where(meta == ef, dr[0:1, :], 0.0)
+            return carry
+
+        lax.fori_loop(0, n_p, one, 0)
+        gx_ref[o] = gxa_ref[...].astype(BF16)
+
+    def sums_out(way):
+        dev = {"fsdp": z + 1 - 2 * way}
+        return (remote(dr_ref.at[1], dr_out, s_gx.at[0], r_gx.at[0], dev),
+                remote(gx_ref.at[1], gx_out, s_gx.at[1], r_gx.at[1], dev))
+
+    n_steps = len(END_STEPS)
+
+    def chosen(of, k):
+        return jnp.where(mid, pick([of(t) for t in MID_STEPS], k), pick([of(t) for t in END_STEPS], k))
 
     def step(k, carry):
         for n in range(n_steps):
-            @pl.when(k == n)
-            def _():
-                with jax.named_scope(f"events_{n}"):
-                    events(n)
-
-        packed = pick([t[0] for t in STEPS], k)
+            @pl.when((k == n) & mid)
+            def _():
+                with jax.named_scope(f"mid_{n}"):
+                    mid_events(n)
+
+            @pl.when((k == n) & jnp.logical_not(mid))
+            def _():
+                with jax.named_scope(f"end_{n}"):
+                    end_events(n)
+
+        packed = chosen(lambda t: t[0], k)
 
         @pl.when(packed >= 0)
         def _():
             j = plane_of(packed)
             with jax.named_scope("landed"):
                 landed(j)
-            with jax.named_scope("compact"):
-                compact(packed, j)
-
-        def chunk_own(c, carry):
-            with jax.named_scope("cells_own"):
-                cells(0, c, True)
+
+            @pl.when(mid & (packed < 2))
+            def _():
+                with jax.named_scope("compact"):
+                    compact(packed, j, True)
+
+            @pl.when(jnp.logical_not(mid & (packed < 2)))
+            def _():
+                with jax.named_scope("compact"):
+                    compact(packed, j, False)
+
+        @pl.when(mid & (k == GATHER_STEP))
+        def _():
+            with jax.named_scope("gather"):
+                gather(1)
+            for way in (0, 1):
+                @pl.when((z == 2) if way == 0 else (z == 1))
+                def _():
+                    start_all(sums_out(way))
+
+        def dx_plane(m, carry):
+            o = 1 - m
+
+            def chunk(c, carry):
+                with jax.named_scope("cells_own"):
+                    cells(o, c, True)
+                return carry
+
+            lo = pick([chosen(lambda t, n=n: t[1 + n][0], k) for n in range(2)], o)
+            hi = pick([chosen(lambda t, n=n: t[1 + n][1], k) for n in range(2)], o)
+            lax.fori_loop(lo, hi, chunk, 0)
+
+            @pl.when(k == SEND_STEP)
+            def _():
+                with jax.named_scope("send_back"):
+                    send_back(o)
+
             return carry
 
-        lax.fori_loop(pick([t[1][0] for t in STEPS], k), pick([t[1][1] for t in STEPS], k), chunk_own, 0)
-
-        @pl.when(k == n_steps - 1)
-        def _():
-            with jax.named_scope("send_back"):
-                send_back()
+        lax.fori_loop(0, jnp.where(mid, 2, 0), dx_plane, 0)
 
         def plane(o, carry):
             def chunk(c, carry):
@@ -442,11 +539,11 @@
                     cells(o, c, False)
                 return carry
 
-            lo = sum(jnp.where(o == n, pick([t[1 + n][0] for t in STEPS], k), 0) for n in range(1, n_z))
-            hi = sum(jnp.where(o == n, pick([t[1 + n][1] for t in STEPS], k), 0) for n in range(1, n_z))
+            lo = pick([chosen(lambda t, n=n: t[1 + n][0], k) for n in range(n_z)], o)
+            hi = pick([chosen(lambda t, n=n: t[1 + n][1], k) for n in range(n_z)], o)
             return lax.fori_loop(lo, hi, chunk, carry)
 
-        return lax.fori_loop(1, n_z, plane, carry)
+        return lax.fori_loop(jnp.where(mid, 2, 0), n_z, plane, carry)
 
     lax.fori_loop(0, n_steps, step, 0)
 
@@ -457,20 +554,39 @@
         dw2_ref[c * fc:(c + 1) * fc, :] = dwt_ref[:, c * fc:(c + 1) * fc].T
     for c in stores:
         c.start()
-    with jax.named_scope("back_wait"):
-        for q in range(1, n_p):
-            frm = flip(p, q)
-            remote(drs_ref.at[frm], drr_ref.at[frm], s_dr.at[frm], r_dr.at[frm], {"ep": frm}).wait_recv()
-            remote(dxs_ref.at[frm], dxr_ref.at[frm], s_dx.at[frm], r_dx.at[frm], {"ep": frm}).wait_recv()
-        for c in own_back():
+
+    @pl.when(mid)
+    def _():
+        with jax.named_scope("gather"):
+            gather(0)
+        own_sums = (pltpu.make_async_copy(gx_ref.at[0], gx_out, s_loc.at[3]),
+                    pltpu.make_async_copy(dr_ref.at[0], dr_out, s_loc.at[4]))
+        start_all(own_sums)
+        for c in own_sums:
             c.wait()
+        for way in (0, 1):
+            @pl.when((z == 2) if way == 0 else (z == 1))
+            def _():
+                for c in sums_out(way):
+                    c.wait_send()
+
+    @pl.when(jnp.logical_not(mid))
+    def _():
+        with jax.named_scope("sums_wait"):
+            for c in sums_out(0):
+                c.wait_recv()
+
     for c in stores:
         c.wait()
 
     with jax.named_scope("drain"):
-        for q in range(1, n_p):
-            for c in back_copy(flip(p, q)):
-                c.wait_send()
+        @pl.when(mid)
+        def _():
+            for o in range(2):
+                for q in range(1, n_p):
+                    for c in back_copy(o, flip(p, q)):
+                        c.wait_send()
+
         for i in range(4):
             for j in range(n_z):
                 for c in plane_copy(j, i):
@@ -496,41 +612,20 @@
                     lax.fori_loop(0, CHUNKS, drain, 0)
 
 
-def finish(cap, n_p, ids_ref, dxr_hbm, drr_hbm, dw0_in, dw1_in, dw2_in,
-           gx_ref, dr_ref, dw0_out, dw1_out, dw2_out,
-           dxr_ref, drr_ref, dw0_ref, dw1_ref, dw2_ref, gxa_ref, s_in, s_out):
-    n_tok = ids_ref.shape[1]
-    rows_in = (pltpu.make_async_copy(dxr_hbm, dxr_ref, s_in.at[0]),
-               pltpu.make_async_copy(drr_hbm, drr_ref, s_in.at[1]))
+def finish(gx_in, dr_ref, dw0_in, dw1_in, dw2_in, gx_out, drt_ref, dw0_out, dw1_out, dw2_out,
+           gx_ref, dw0_ref, dw1_ref, dw2_ref, s_in, s_out):
     moves = tuple(
-        (pltpu.make_async_copy(src, mid, s_in.at[2 + n]), pltpu.make_async_copy(mid, dst, s_out.at[n]))
+        (pltpu.make_async_copy(src, mid, s_in.at[n]), pltpu.make_async_copy(mid, dst, s_out.at[n]))
         for n, (src, mid, dst) in enumerate(
-            ((dw0_in, dw0_ref, dw0_out), (dw1_in, dw1_ref, dw1_out), (dw2_in, dw2_ref, dw2_out))))
-    for c in rows_in:
-        c.start()
+            ((gx_in, gx_ref, gx_out), (dw0_in, dw0_ref, dw0_out), (dw1_in, dw1_ref, dw1_out),
+             (dw2_in, dw2_ref, dw2_out))))
     for c, _ in moves:
         c.start()
-    ids = ids_ref[...].astype(F32)
-    pos16 = positions(ids, earlier(n_tok), cap)
-    gxa_ref[...] = jnp.zeros_like(gxa_ref)
-    dr_ref[...] = jnp.zeros_like(dr_ref)
-    for c in rows_in:
-        c.wait()
+    drt_ref[0:1, :] = dr_ref[0:1, :]
+    drt_ref[1:2, :] = dr_ref[1:2, :]
     for c_in, c_out in moves:
         c_in.wait()
         c_out.start()
-
-    def gather(e, carry):
-        ef = e.astype(F32)
-        pos = pick_row(pos16, ef)
-        hit = jnp.where(iota_f32((cap, n_tok), 0) == pos, 1.0, 0.0).astype(BF16)
-        gxa_ref[...] += dot_tn(hit, dxr_ref[e])
-        dr = drr_ref[e]
-        dr_ref[...] += jnp.where(ids == ef, dr[0:1, :], 0.0)
-        return carry
-
-    lax.fori_loop(0, n_p, gather, 0)
-    gx_ref[...] = gxa_ref[...].astype(BF16)
     for _, c in moves:
         c.wait()
 
@@ -556,7 +651,7 @@
         dw_shapes = (out((dl, f), F32), out((dl, f), F32), out((f, dl), F32))
         back = pl.pallas_call(
             functools.partial(kernel, cap, n_z, n_p),
-            out_shape=(out((n_p, cap, d), BF16), out((n_p, 8, n_tok), F32)) + dw_shapes,
+            out_shape=(out((n_tok, d), BF16), out((8, n_tok), F32)) + dw_shapes,
             in_specs=[vmem] * 2 + [hbm] * 5,
             out_specs=(hbm,) * 5,
             scratch_shapes=[
@@ -566,13 +661,18 @@
                 pltpu.VMEM((n_tok, n_tok), BF16),
                 pltpu.VMEM((n_t, rows, d), BF16),
                 pltpu.VMEM((n_t, rows, d), BF16),
-                pltpu.VMEM((n_p // 4, rows, d), BF16),
+                pltpu.VMEM((2, n_p // 4, rows, d), BF16),
                 pltpu.VMEM((n_t, dl, rows), BF16),
                 pltpu.VMEM((n_t, dl, rows), BF16),
-                pltpu.VMEM((n_p // 4, rows, min(128, d)), F32),
-                pltpu.VMEM((n_p // 4, rows, d), F32),
-                pltpu.VMEM((n_p, cap, d), BF16),
-                pltpu.VMEM((n_p, 8, n_tok), F32),
+                pltpu.VMEM((2, n_p // 4, rows, min(128, d)), F32),
+                pltpu.VMEM((2, n_p // 4, rows, d), F32),
+                pltpu.VMEM((2, n_p, cap, d), BF16),
+                pltpu.VMEM((2, n_p, 8, n_tok), F32),
+                pltpu.VMEM((2, n_p, cap, d), BF16),
+                pltpu.VMEM((2, n_p, 8, n_tok), F32),
+                pltpu.VMEM((n_tok, d), F32),
+                pltpu.VMEM((2, n_tok, d), BF16),
+                pltpu.VMEM((2, 8, n_tok), F32),
                 pltpu.VMEM((dl, f), F32),
                 pltpu.VMEM((dl, f), F32),
                 pltpu.VMEM((dl, f), F32),
@@ -582,27 +682,25 @@
                 sem((2, n_z, CHUNKS)), sem((n_z, CHUNKS)),
                 sem((n_z, 4)), sem((n_z, n_p)), sem((n_z, 4)), sem((n_z, n_p)),
                 sem((n_z, 3)), sem((n_z, 3)),
-                sem((n_p,)), sem((n_p,)), sem((n_p,)), sem((n_p,)),
+                sem((2, n_p)), sem((2, n_p)), sem((2, n_p)), sem((2, n_p)), sem((2,)), sem((2,)),
                 sem((5,)),
             ],
             compiler_params=pltpu.CompilerParams(
                 collective_id=0, has_side_effects=True, vmem_limit_bytes=67043328),
         )(ids, rw, x_tok, dy_tok, w_gate, w_up, w_down)
         gx, dr, dw0, dw1, dw2 = pl.pallas_call(
-            functools.partial(finish, cap, n_p),
+            finish,
             out_shape=(out((n_tok, d), BF16), out((top_k, n_tok), F32)) + dw_shapes,
-            in_specs=[vmem] + [hbm] * 5,
-            out_specs=(vmem,) * 2 + (hbm,) * 3,
+            in_specs=[hbm, vmem] + [hbm] * 3,
+            out_specs=(hbm, vmem) + (hbm,) * 3,
             scratch_shapes=[
-                pltpu.VMEM((n_p, cap, d), BF16),
-                pltpu.VMEM((n_p, 8, n_tok), F32),
+                pltpu.VMEM((n_tok, d), BF16),
                 pltpu.VMEM((dl, f), F32),
                 pltpu.VMEM((dl, f), F32),
                 pltpu.VMEM((f, dl), F32),
-                pltpu.VMEM((n_tok, d), F32),
-                sem((5,)), sem((3,)),
+                sem((4,)), sem((4,)),
             ],
-        )(ids, *back)
+        )(*back)
         return gx, dr.T, dw0[None], dw1[None], dw2[None]
 
     return jax.shard_map(

time: 161 us -> 157 us (0.975)
  the two profiles are of different devices: /device:TPU:0 before, /device:TPU:8 now
where the time goes in v4:
time: 157 us
  Pallas kernels  156 us (99%)
    pallas_call x1, Pallas kernels, per_device(): pl.pallas_call(functools.partial(kernel, cap, n_z, n_p), out_shape=(out((...  152 us
    pallas_call x1, Pallas kernels, per_device(): pl.pallas_call(finish, out_shape=(out((n_tok, d), BF16), out((top_k, n_to...  4.14 us

profile of v4, /device:TPU:8, one launch (start us, length us, event | category | flops | bytes accessed | tf_op | source)
XLA Modules:
  0.0 156.6 jit_solution(7363412713443539007)
XLA Ops:
  0.6 151.8 %shard_map.110 = (bf16[256,512]{1,0:T(8,128)(2,1)}, f32[8,256]{1,0:T(8,128)}, f32[128,1792]{1,0:T(8,128)}, f32[128,1792]{1,0:T(8,128)}, f32[1792,128]{1,0:T(8,128)}) custom-call(s32[2,256]{1,0:T(2,128)} %bitcast.6, f32[2,256]{1,0:T(2,128)} %bitcast.7, bf16[256,512]{1,0:T(8,128)(2,1)} %x_ref.1, bf16[256,512]{1,0:T(8,128)(2,1)} %dy_ref.1, ...), custom_call_target="tpu_custom_call" | custom-call | tf_op jit(solution)/shard_map/pallas_call | solution.py:652
  152.5 4.1 %shard_map.111 = (bf16[256,512]{1,0:T(8,128)(2,1)}, f32[2,256]{1,0:T(2,128)}, f32[128,1792]{1,0:T(8,128)}, f32[128,1792]{1,0:T(8,128)}, f32[1792,128]{1,0:T(8,128)}) custom-call(bf16[256,512]{1,0:T(8,128)(2,1)} %get-tuple-element.15.gx_in, f32[8,256]{1,0:T(8,128)} %get-tuple-element.16.dr_ref, f32[128,1792]{1,0:T(8,128)} %get-tuple-element.17.dw0_in, ...), custom_call_target="tpu_custom_call" | custom-call | tf_op jit(solution)/shard_map/pallas_call | solution.py:691

commit v5 on v4

--- a/solution.py
+++ b/solution.py
@@ -17,35 +17,34 @@
 SUB = 3
 RETURN = (6, 4, 7, 5, 2, 3, 1, 0)
 ORDER = ((0, 1, 2, 3), (1, 0, 2, 3), (2, 3, 1, 0), (3, 2, 1, 0))
+SKIP = -1
 NONE = (0, 0)
+PAIR = (0, 2)
+FULL = (0, CHUNKS)
+ONE = tuple((c, c + 1) for c in range(CHUNKS))
 END_STEPS = (
     (0, NONE, NONE, NONE, NONE),
-    (-1, (0, 1), NONE, NONE, NONE),
-    (1, NONE, (0, 1), NONE, NONE),
-    (-1, (1, 2), (1, 2), NONE, NONE),
-    (2, NONE, NONE, (0, 2), NONE),
-    (-1, (2, 3), (2, 3), (2, 3), NONE),
-    (-1, (3, 4), (3, 4), (3, 4), NONE),
+    (SKIP, ONE[0], NONE, NONE, NONE),
+    (1, ONE[1], PAIR, NONE, NONE),
+    (SKIP, NONE, NONE, NONE, NONE),
+    (2, NONE, NONE, PAIR, NONE),
+    (SKIP, ONE[2], ONE[2], ONE[2], NONE),
+    (SKIP, ONE[3], ONE[3], ONE[3], NONE),
     (3, NONE, NONE, NONE, (0, 4)),
-    (-1, (4, 5), (4, 5), (4, 5), (4, 5)),
-    (-1, (5, 6), (5, 6), (5, 6), (5, 6)),
-    (-1, (6, 7), (6, 7), (6, 7), (6, 7)),
+) + tuple((SKIP, c, c, c, c) for c in ONE[4:])
+MID_STEPS = (
+    (0, ONE[0], NONE, NONE, NONE),
+    (SKIP, ONE[1], NONE, NONE, NONE),
+    (SKIP, ONE[2], NONE, NONE, NONE),
+    (1, NONE, PAIR, NONE, NONE),
+    (SKIP, ONE[3], (2, 4), NONE, NONE),
+) + tuple((SKIP, c, c, NONE, NONE) for c in ONE[4:]) + (
+    (2, NONE, NONE, FULL, NONE),
+    (3, NONE, NONE, NONE, NONE),
+    (SKIP, NONE, NONE, NONE, FULL),
 )
-MID_STEPS = (
-    (0, (0, 1), NONE, NONE, NONE),
-    (-1, (1, 2), NONE, NONE, NONE),
-    (1, (2, 3), (0, 1), NONE, NONE),
-    (-1, (3, 4), (1, 4), NONE, NONE),
-    (-1, (4, 5), (4, 5), NONE, NONE),
-    (-1, (5, 6), (5, 6), NONE, NONE),
-    (-1, (6, 7), (6, 7), NONE, NONE),
-    (2, NONE, NONE, (0, 7), NONE),
-    (3, NONE, NONE, NONE, NONE),
-    (-1, NONE, NONE, NONE, (0, 7)),
-    (-1, NONE, NONE, NONE, NONE),
-)
-SEND_STEP = 6
-GATHER_STEP = 9
+SEND_STEP = 7
+GATHER_STEP = 10
 
 
 def capacity_of(tok_dev, top_k, experts):
@@ -206,15 +205,25 @@
                     for c in chunks:
                         w_copy(z, c, way).start()
 
-    def pass_w(q, dist, c):
+    def pass_w(q, dist, c, wait=True, send=True):
         for way in (0, 1):
             there, depth = link(way)
 
             @pl.when(there & (depth == q))
             def _():
                 j = upstream(way, dist)
-                w_copy(j, c, way).wait_recv()
-                w_copy(j, c, way).start()
+                if wait:
+                    w_copy(j, c, way).wait_recv()
+                if send:
+                    w_copy(j, c, way).start()
+
+    def pass_tokens(q, dist):
+        for way in (0, 1):
+            there, depth = link(way)
+
+            @pl.when(there & (depth == q))
+            def _():
+                start_all(zt_copy(upstream(way, dist), way))
 
     def need_w(c):
         for way in (0, 1):
@@ -228,7 +237,7 @@
 
     def tokens(dist):
         for way, turn in ((0, z < 2), (1, z >= 0), (0, z >= 2)):
-            there, _ = link(way)
+            there, depth = link(way)
             j = upstream(way, dist)
 
             @pl.when(turn & valid_z(j))
@@ -236,7 +245,7 @@
                 for c in zt_copy(j, way):
                     c.wait_recv()
 
-                @pl.when(there)
+                @pl.when(there & (depth == n_z - 2))
                 def _():
                     start_all(zt_copy(j, way))
 
@@ -268,6 +277,7 @@
             start_all(zt_copy(z, way))
     for i in range(4):
         start_all(plane_copy(z, i))
+    own_w((1,), (1,))
     own_w((0,), range(1, CHUNKS))
     tri_ref[...] = earlier(n_tok)
     for ref in (dw0_ref, dw1_ref, dwt_ref, dy_y_ref, dx_ref):
@@ -282,9 +292,9 @@
             need_w(0)
         elif k == 2:
             relay(1)
+            need_w(1)
+        elif k == 3:
             tokens(3)
-        elif k == 3:
-            need_w(1)
         elif k == 4:
             relay(2)
         elif k in (5, 6):
@@ -299,28 +309,35 @@
             pass_w(1, 1, 0)
             pass_w(2, 1, 0)
             tokens(1)
+            pass_w(1, 1, 1)
+            own_w((1,), (2,))
+            relay(0)
+            pass_w(1, 1, 2)
+            pass_tokens(1, 1)
             pass_w(2, 2, 0)
-            batch(1, 1)
-            relay(0)
         elif k == 1:
+            batch(2, 1)
+            batch(1, 3)
+        elif k == 2:
+            own_w((2,), (2,))
+            pass_w(2, 1, 2, send=False)
+            pass_w(2, 2, 2, send=False)
+        elif k == 3:
+            relay(1)
             tokens(2)
-            batch(1, 2)
-            batch(2, 1)
-        elif k == 2:
-            batch(1, 3)
-            relay(1)
-            batch(2, 2)
-        elif k == 3:
-            batch(2, 3)
+            pass_w(2, 1, 2, wait=False)
+            pass_w(2, 2, 2, wait=False)
             batch(1, 4)
             batch(1, 5)
             batch(1, 6)
         elif k == 4:
+            batch(2, 3)
+        elif k == 5:
+            batch(2, 4)
             relay(2)
-            batch(2, 4)
-        elif k in (5, 6):
-            batch(2, k)
-        elif k == 7:
+        elif k in (6, 7):
+            batch(2, k - 1)
+        elif k == 8:
             relay(3)
 
     def rows_of(s):
@@ -344,7 +361,7 @@
                 dyc_ref[o, h, rows, :] = dy.astype(BF16)
             return carry
 
-        lax.fori_loop(0, n_p, one, 0, unroll=2)
+        lax.fori_loop(0, n_p, one, 0, unroll=4)
 
         def turn(h, carry):
             xt_ref[o * n_h + h] = xc_ref[o * n_h + h, :, own_rows].T
@@ -406,7 +423,7 @@
             def _():
                 start_all(own_back(o))
 
-        def one(n, carry):
+        def one(n):
             s = flip(p, pick(RETURN, n))
             h, rows = rows_of(s)
             dxs_ref[o, s] = dx_ref[o, h, rows, :].astype(BF16)
@@ -416,13 +433,19 @@
             dr_row = jnp.sum(jnp.where(hit, dr_col, 0.0), axis=0, keepdims=True)
             drs_ref[o, s] = jnp.broadcast_to(dr_row, (8, n_tok))
 
+        def pair(n, carry):
+            one(2 * n)
+            one(2 * n + 1)
+
             @pl.when(n > 0)
             def _():
-                leave(n - 1)
+                leave(2 * n - 2)
+                leave(2 * n - 1)
 
             return carry
 
-        lax.fori_loop(0, n_p, one, 0)
+        lax.fori_loop(0, n_p // 2, pair, 0)
+        leave(n_p - 2)
         leave(n_p - 1)
 
     def back_copy(o, to):
@@ -439,19 +462,14 @@
         gxa_ref[...] = jnp.zeros_like(gxa_ref)
         dr_ref[o] = jnp.zeros_like(dr_ref[o])
 
-        def one(n, carry):
-            e = flip(p, pick(RETURN, n))
-
-            @pl.when(e != p)
-            def _():
-                remote(drs_ref.at[o, e], drr_ref.at[o, e], s_dr.at[o, e], r_dr.at[o, e], {"ep": e}).wait_recv()
-                remote(dxs_ref.at[o, e], dxr_ref.at[o, e], s_dx.at[o, e], r_dx.at[o, e], {"ep": e}).wait_recv()
-
-            @pl.when(e == p)
-            def _():
-                for c in own_back(o):
-                    c.wait()
-
+        for q in range(1, n_p):
+            e = flip(p, q)
+            remote(drs_ref.at[o, e], drr_ref.at[o, e], s_dr.at[o, e], r_dr.at[o, e], {"ep": e}).wait_recv()
+            remote(dxs_ref.at[o, e], dxr_ref.at[o, e], s_dx.at[o, e], r_dx.at[o, e], {"ep": e}).wait_recv()
+        for c in own_back(o):
+            c.wait()
+
+        def one(e, carry):
             ef = e.astype(F32)
             pos = pick_row(pos16, ef)
             hit = jnp.where(iota_f32((cap, n_tok), 0) == pos, 1.0, 0.0).astype(BF16)
@@ -460,7 +478,7 @@
             dr_ref[o] += jnp.where(meta == ef, dr[0:1, :], 0.0)
             return carry
 
-        lax.fori_loop(0, n_p, one, 0)
+        lax.fori_loop(0, n_p, one, 0, unroll=4)
         gx_ref[o] = gxa_ref[...].astype(BF16)
 
     def sums_out(way):

time: 157 us -> 148 us (0.943)
  the two profiles are of different devices: /device:TPU:8 before, /device:TPU:0 now
where the time goes in v5:
time: 148 us
  Pallas kernels  148 us (100%)
    pallas_call x1, Pallas kernels, per_device(): pl.pallas_call(functools.partial(kernel, cap, n_z, n_p), out_shape=(out((...  143 us
    pallas_call x1, Pallas kernels, per_device(): pl.pallas_call(finish, out_shape=(out((n_tok, d), BF16), out((top_k, n_to...  4.14 us

profile of v5, /device:TPU:0, one launch (start us, length us, event | category | flops | bytes accessed | tf_op | source)
XLA Modules:
  0.0 148.2 jit_solution(935599941320374307)
XLA Ops:
  0.6 143.4 %shard_map.110 = (bf16[256,512]{1,0:T(8,128)(2,1)}, f32[8,256]{1,0:T(8,128)}, f32[128,1792]{1,0:T(8,128)}, f32[128,1792]{1,0:T(8,128)}, f32[1792,128]{1,0:T(8,128)}) custom-call(s32[2,256]{1,0:T(2,128)} %bitcast.6, f32[2,256]{1,0:T(2,128)} %bitcast.7, bf16[256,512]{1,0:T(8,128)(2,1)} %x_ref.1, bf16[256,512]{1,0:T(8,128)(2,1)} %dy_ref.1, ...), custom_call_target="tpu_custom_call" | custom-call | tf_op jit(solution)/shard_map/pallas_call | solution.py:670
  144.0 4.1 %shard_map.111 = (bf16[256,512]{1,0:T(8,128)(2,1)}, f32[2,256]{1,0:T(2,128)}, f32[128,1792]{1,0:T(8,128)}, f32[128,1792]{1,0:T(8,128)}, f32[1792,128]{1,0:T(8,128)}) custom-call(bf16[256,512]{1,0:T(8,128)(2,1)} %get-tuple-element.15.gx_in, f32[8,256]{1,0:T(8,128)} %get-tuple-element.16.dr_ref, f32[128,1792]{1,0:T(8,128)} %get-tuple-element.17.dw0_in, ...), custom_call_target="tpu_custom_call" | custom-call | tf_op jit(solution)/shard_map/pallas_call | solution.py:709

commit v6 on v5

--- a/solution.py
+++ b/solution.py
@@ -15,6 +15,7 @@
 DIAG = (2, 4, 6)
 DIRECT = (1, 2, 4, 6)
 SUB = 3
+PIECES = 4
 RETURN = (6, 4, 7, 5, 2, 3, 1, 0)
 ORDER = ((0, 1, 2, 3), (1, 0, 2, 3), (2, 3, 1, 0), (3, 2, 1, 0))
 SKIP = -1
@@ -102,9 +103,9 @@
            gx_out, dr_out, dw0_out, dw1_out, dw2_out,
            xd_all, meta_all, w_all, tri_ref, xc_ref, gc_ref, dyc_ref, xt_ref, gt_ref, dy_y_ref, dx_ref,
            dxs_ref, drs_ref, dxr_ref, drr_ref, gxa_ref, gx_ref, dr_ref,
-           dw0_ref, dw1_ref, dwt_ref, dw2_ref, wd_own,
+           dw0_ref, dw1_ref, dwt_ref, dw2_ref, wd_own, ids_own, rw_own,
            s_zt, r_zt, s_zm, r_zm, s_w, r_w, s_p, r_p, s_pm, r_pm, s_r, s_rm,
-           s_dx, r_dx, s_dr, r_dr, s_gx, r_gx, s_loc):
+           s_dx, r_dx, s_dr, r_dr, s_gx, r_gx, s_dw, s_loc):
     z = lax.axis_index("fsdp")
     p = lax.axis_index("ep")
     e_mine = p.astype(F32)
@@ -139,11 +140,15 @@
         pltpu.make_async_copy(x_ref, xd_all.at[z, p, :, pl.ds(0, d)], s_loc.at[0]),
         pltpu.make_async_copy(dy_ref, xd_all.at[z, p, :, pl.ds(d, d)], s_loc.at[1]),
     )
+    small = (pltpu.make_async_copy(ids_ref, ids_own, s_loc.at[5]),
+             pltpu.make_async_copy(rw_ref, rw_own, s_loc.at[6]))
     load_wd.start()
-    for c in loads:
+    for c in small + loads:
         c.start()
-    meta_all[z, p, 0:2, :] = ids_ref[...].astype(F32)
-    meta_all[z, p, 2:4, :] = rw_ref[...]
+    for c in small:
+        c.wait()
+    meta_all[z, p, 0:2, :] = ids_own[...].astype(F32)
+    meta_all[z, p, 2:4, :] = rw_own[...]
     meta_all[z, p, 4:8, :] = jnp.zeros((4, n_tok), F32)
     load_wd.wait()
     for c in range(CHUNKS):
@@ -488,6 +493,12 @@
 
     n_steps = len(END_STEPS)
 
+    def stores(c):
+        cols = pl.ds(pl.multiple_of(c * fc, fc), fc)
+        return (pltpu.make_async_copy(dw0_ref.at[:, cols], dw0_out.at[:, cols], s_dw.at[0, c]),
+                pltpu.make_async_copy(dw1_ref.at[:, cols], dw1_out.at[:, cols], s_dw.at[1, c]),
+                pltpu.make_async_copy(dw2_ref.at[cols, :], dw2_out.at[cols, :], s_dw.at[2, c]))
+
     def chosen(of, k):
         return jnp.where(mid, pick([of(t) for t in MID_STEPS], k), pick([of(t) for t in END_STEPS], k))
 
@@ -555,6 +566,13 @@
             def chunk(c, carry):
                 with jax.named_scope("cells"):
                     cells(o, c, False)
+
+                @pl.when(o == n_z - 1)
+                def _():
+                    cols = pl.ds(pl.multiple_of(c * fc, fc), fc)
+                    dw2_ref[cols, :] = dwt_ref[:, cols].T
+                    start_all(stores(c))
+
                 return carry
 
             lo = pick([chosen(lambda t, n=n: t[1 + n][0], k) for n in range(n_z)], o)
@@ -564,14 +582,6 @@
         return lax.fori_loop(jnp.where(mid, 2, 0), n_z, plane, carry)
 
     lax.fori_loop(0, n_steps, step, 0)
-
-    stores = [pltpu.make_async_copy(dw0_ref, dw0_out, s_loc.at[0]),
-              pltpu.make_async_copy(dw1_ref, dw1_out, s_loc.at[1]),
-              pltpu.make_async_copy(dw2_ref, dw2_out, s_loc.at[2])]
-    for c in range(CHUNKS):
-        dw2_ref[c * fc:(c + 1) * fc, :] = dwt_ref[:, c * fc:(c + 1) * fc].T
-    for c in stores:
-        c.start()
 
     @pl.when(mid)
     def _():
@@ -594,8 +604,12 @@
             for c in sums_out(0):
                 c.wait_recv()
 
-    for c in stores:
-        c.wait()
+    def stored(c, carry):
+        for copy in stores(c):
+            copy.wait()
+        return carry
+
+    lax.fori_loop(0, CHUNKS, stored, 0)
 
     with jax.named_scope("drain"):
         @pl.when(mid)
@@ -630,22 +644,30 @@
                     lax.fori_loop(0, CHUNKS, drain, 0)
 
 
-def finish(gx_in, dr_ref, dw0_in, dw1_in, dw2_in, gx_out, drt_ref, dw0_out, dw1_out, dw2_out,
-           gx_ref, dw0_ref, dw1_ref, dw2_ref, s_in, s_out):
-    moves = tuple(
-        (pltpu.make_async_copy(src, mid, s_in.at[n]), pltpu.make_async_copy(mid, dst, s_out.at[n]))
-        for n, (src, mid, dst) in enumerate(
-            ((gx_in, gx_ref, gx_out), (dw0_in, dw0_ref, dw0_out), (dw1_in, dw1_ref, dw1_out),
-             (dw2_in, dw2_ref, dw2_out))))
+def finish(gx_in, dr_in, dw0_in, dw1_in, dw2_in, gx_out, dr_out, dw0_out, dw1_out, dw2_out,
+           gx_ref, dr_ref, drt_ref, dw0_ref, dw1_ref, dw2_ref, s_in, s_out):
+    moves = []
+    for src, via, dst in ((dw0_in, dw0_ref, dw0_out), (dw1_in, dw1_ref, dw1_out), (dw2_in, dw2_ref, dw2_out),
+                          (gx_in, gx_ref, gx_out)):
+        rows = src.shape[0] // PIECES
+        for at in [pl.ds(i * rows, rows) for i in range(PIECES)]:
+            n = len(moves)
+            moves.append((pltpu.make_async_copy(src.at[at, :], via.at[at, :], s_in.at[n]),
+                          pltpu.make_async_copy(via.at[at, :], dst.at[at, :], s_out.at[n])))
+    dr_load = pltpu.make_async_copy(dr_in, dr_ref, s_in.at[len(moves)])
+    dr_store = pltpu.make_async_copy(drt_ref, dr_out, s_out.at[len(moves)])
+    dr_load.start()
     for c, _ in moves:
         c.start()
-    drt_ref[0:1, :] = dr_ref[0:1, :]
-    drt_ref[1:2, :] = dr_ref[1:2, :]
+    dr_load.wait()
+    drt_ref[...] = dr_ref[: drt_ref.shape[0], :]
     for c_in, c_out in moves:
         c_in.wait()
         c_out.start()
+    dr_store.start()
     for _, c in moves:
         c.wait()
+    dr_store.wait()
 
 
 def solution(mesh):
@@ -662,7 +684,6 @@
         rows = 4 * cap
         n_t = n_z * n_p // 4
         sem = pltpu.SemaphoreType.DMA
-        vmem = pl.BlockSpec(memory_space=pltpu.VMEM)
         hbm = pl.BlockSpec(memory_space=pl.ANY)
         out = jax.ShapeDtypeStruct
         ids, rw = expert_ids.T, route_w.T
@@ -670,7 +691,7 @@
         back = pl.pallas_call(
             functools.partial(kernel, cap, n_z, n_p),
             out_shape=(out((n_tok, d), BF16), out((8, n_tok), F32)) + dw_shapes,
-            in_specs=[vmem] * 2 + [hbm] * 5,
+            in_specs=[hbm] * 7,
             out_specs=(hbm,) * 5,
             scratch_shapes=[
                 pltpu.VMEM((n_z, n_p, n_tok, 2 * d), BF16),
@@ -696,12 +717,15 @@
                 pltpu.VMEM((dl, f), F32),
                 pltpu.VMEM((f, dl), F32),
                 pltpu.VMEM((f, dl), BF16),
+                pltpu.VMEM((top_k, n_tok), jnp.int32),
+                pltpu.VMEM((top_k, n_tok), F32),
                 sem((2, n_z)), sem((n_z,)), sem((2, n_z)), sem((n_z,)),
                 sem((2, n_z, CHUNKS)), sem((n_z, CHUNKS)),
                 sem((n_z, 4)), sem((n_z, n_p)), sem((n_z, 4)), sem((n_z, n_p)),
                 sem((n_z, 3)), sem((n_z, 3)),
                 sem((2, n_p)), sem((2, n_p)), sem((2, n_p)), sem((2, n_p)), sem((2,)), sem((2,)),
-                sem((5,)),
+                sem((3, CHUNKS)),
+                sem((7,)),
             ],
             compiler_params=pltpu.CompilerParams(
                 collective_id=0, has_side_effects=True, vmem_limit_bytes=67043328),
@@ -709,14 +733,16 @@
         gx, dr, dw0, dw1, dw2 = pl.pallas_call(
             finish,
             out_shape=(out((n_tok, d), BF16), out((top_k, n_tok), F32)) + dw_shapes,
-            in_specs=[hbm, vmem] + [hbm] * 3,
-            out_specs=(hbm, vmem) + (hbm,) * 3,
+            in_specs=[hbm] * 5,
+            out_specs=(hbm,) * 5,
             scratch_shapes=[
                 pltpu.VMEM((n_tok, d), BF16),
+                pltpu.VMEM((8, n_tok), F32),
+                pltpu.VMEM((top_k, n_tok), F32),
                 pltpu.VMEM((dl, f), F32),
                 pltpu.VMEM((dl, f), F32),
                 pltpu.VMEM((f, dl), F32),
-                sem((4,)), sem((4,)),
+                sem((4 * PIECES + 1,)), sem((4 * PIECES + 1,)),
             ],
         )(*back)
         return gx, dr.T, dw0[None], dw1[None], dw2[None]

time: 148 us -> 147 us (level)
  Pallas kernels: 148 us -> 145 us
where the time goes in v6:
time: 147 us; the launch traced here: 146 us
  Pallas kernels  145 us (99%)
    pallas_call x1, Pallas kernels, per_device(): pl.pallas_call(functools.partial(kernel, cap, n_z, n_p), out_shape=(out((...  142 us
    pallas_call x1, Pallas kernels, per_device(): pl.pallas_call(finish, out_shape=(out((n_tok, d), BF16), out((top_k, n_to...  2.99 us

profile of v6, /device:TPU:0, one launch (start us, length us, event | category | flops | bytes accessed | tf_op | source)
XLA Modules:
  0.0 145.8 jit_solution(16536997920960712730)
XLA Ops:
  0.6 142.2 %shard_map.110 = (bf16[256,512]{1,0:T(8,128)(2,1)}, f32[8,256]{1,0:T(8,128)}, f32[128,1792]{1,0:T(8,128)}, f32[128,1792]{1,0:T(8,128)}, f32[1792,128]{1,0:T(8,128)}) custom-call(s32[2,256]{1,0:T(2,128)} %bitcast.6, f32[2,256]{1,0:T(2,128)} %bitcast.7, bf16[256,512]{1,0:T(8,128)(2,1)} %x_ref.1, bf16[256,512]{1,0:T(8,128)(2,1)} %dy_ref.1, ...), custom_call_target="tpu_custom_call" | custom-call | tf_op jit(solution)/shard_map/pallas_call | solution.py:691
  142.8 3.0 %shard_map.111 = (bf16[256,512]{1,0:T(8,128)(2,1)}, f32[2,256]{1,0:T(2,128)}, f32[128,1792]{1,0:T(8,128)}, f32[128,1792]{1,0:T(8,128)}, f32[1792,128]{1,0:T(8,128)}) custom-call(bf16[256,512]{1,0:T(8,128)(2,1)} %get-tuple-element.15.gx_in, f32[8,256]{1,0:T(8,128)} %get-tuple-element.16.dr_in, f32[128,1792]{1,0:T(8,128)} %get-tuple-element.17.dw0_in, ...), custom_call_target="tpu_custom_call" | custom-call | tf_op jit(solution)/shard_map/pallas_call | solution.py:733

commit v7 on v6

--- a/solution.py
+++ b/solution.py
@@ -16,6 +16,8 @@
 DIRECT = (1, 2, 4, 6)
 SUB = 3
 PIECES = 4
+EARLY = (0, 1, 2, 3, 4, 5)
+LATE = (6, 7)
 RETURN = (6, 4, 7, 5, 2, 3, 1, 0)
 ORDER = ((0, 1, 2, 3), (1, 0, 2, 3), (2, 3, 1, 0), (3, 2, 1, 0))
 SKIP = -1
@@ -257,16 +259,22 @@
                 for i in range(4):
                     start_all(plane_copy(j, i))
 
-    def relay(o):
+    def relay(o, which=(0, 1, 2)):
         j = plane_of(o)
-        for i, q in enumerate(DIAG):
-            plane_wait(j, flip(p, q))
+        for i in which:
+            plane_wait(j, flip(p, DIAG[i]))
             start_all(relay_copy(j, i))
 
-    def landed(j):
-        plane_wait(j, partner)
-        for q in DIAG:
-            plane_wait(j, flip(partner, q))
+    def landed(j, sources=DIRECT):
+        for q in sources:
+            plane_wait(j, partner if q == 1 else flip(partner, q))
+
+    def early_pack(o):
+        relay(o, (0, 1))
+        landed(plane_of(o), DIRECT[:3])
+        with jax.named_scope("compact_early"):
+            pack(o, plane_of(o), EARLY, 3, True)
+        relay(o, (2,))
 
     def batch(q, c):
         own_w((q,), (c,))
@@ -316,7 +324,7 @@
             tokens(1)
             pass_w(1, 1, 1)
             own_w((1,), (2,))
-            relay(0)
+            early_pack(0)
             pass_w(1, 1, 2)
             pass_tokens(1, 1)
             pass_w(2, 2, 0)
@@ -328,7 +336,7 @@
             pass_w(2, 1, 2, send=False)
             pass_w(2, 2, 2, send=False)
         elif k == 3:
-            relay(1)
+            early_pack(1)
             tokens(2)
             pass_w(2, 1, 2, wait=False)
             pass_w(2, 2, 2, wait=False)
@@ -348,8 +356,9 @@
     def rows_of(s):
         return lax.div(s, per_h), pl.ds(pl.multiple_of(lax.rem(s, per_h) * cap, cap), cap)
 
-    def compact(o, j, keep_dy):
-        def one(s, carry):
+    def pack(o, j, sources, unroll, keep_dy):
+        def one(n, carry):
+            s = flip(p, pick(sources, n))
             meta = meta_all[j, s]
             pos = pick_row(positions(meta, tri_ref[...], cap), e_mine)
             hit = iota_f32((cap, n_tok), 0) == pos
@@ -366,8 +375,9 @@
                 dyc_ref[o, h, rows, :] = dy.astype(BF16)
             return carry
 
-        lax.fori_loop(0, n_p, one, 0, unroll=4)
-
+        lax.fori_loop(0, len(sources), one, 0, unroll=unroll)
+
+    def turned(o):
         def turn(h, carry):
             xt_ref[o * n_h + h] = xc_ref[o * n_h + h, :, own_rows].T
             gt_ref[o * n_h + h] = gc_ref[o * n_h + h, :, own_rows].T
@@ -519,18 +529,19 @@
         @pl.when(packed >= 0)
         def _():
             j = plane_of(packed)
-            with jax.named_scope("landed"):
+            @pl.when(mid & (packed < 2))
+            def _():
+                landed(j, DIRECT[3:])
+                with jax.named_scope("compact"):
+                    pack(packed, j, LATE, 2, True)
+
+            @pl.when(jnp.logical_not(mid & (packed < 2)))
+            def _():
                 landed(j)
-
-            @pl.when(mid & (packed < 2))
-            def _():
                 with jax.named_scope("compact"):
-                    compact(packed, j, True)
-
-            @pl.when(jnp.logical_not(mid & (packed < 2)))
-            def _():
-                with jax.named_scope("compact"):
-                    compact(packed, j, False)
+                    pack(packed, j, EARLY + LATE, 4, False)
+
+            turned(packed)
 
         @pl.when(mid & (k == GATHER_STEP))
         def _():

time: 147 us -> 146 us (level)
  no operation moved by 1% of the time
where the time goes in v7:
time: 146 us
  Pallas kernels  145 us (99%)
    pallas_call x1, Pallas kernels, per_device(): pl.pallas_call(functools.partial(kernel, cap, n_z, n_p), out_shape=(out((...  142 us
    pallas_call x1, Pallas kernels, per_device(): pl.pallas_call(finish, out_shape=(out((n_tok, d), BF16), out((top_k, n_to...  2.99 us

profile of v7, /device:TPU:0, one launch (start us, length us, event | category | flops | bytes accessed | tf_op | source)
XLA Modules:
  0.0 145.8 jit_solution(2691645371884324426)
XLA Ops:
  0.6 142.1 %shard_map.110 = (bf16[256,512]{1,0:T(8,128)(2,1)}, f32[8,256]{1,0:T(8,128)}, f32[128,1792]{1,0:T(8,128)}, f32[128,1792]{1,0:T(8,128)}, f32[1792,128]{1,0:T(8,128)}) custom-call(s32[2,256]{1,0:T(2,128)} %bitcast.6, f32[2,256]{1,0:T(2,128)} %bitcast.7, bf16[256,512]{1,0:T(8,128)(2,1)} %x_ref.1, bf16[256,512]{1,0:T(8,128)(2,1)} %dy_ref.1, ...), custom_call_target="tpu_custom_call" | custom-call | tf_op jit(solution)/shard_map/pallas_call | solution.py:702
  142.8 3.0 %shard_map.111 = (bf16[256,512]{1,0:T(8,128)(2,1)}, f32[2,256]{1,0:T(2,128)}, f32[128,1792]{1,0:T(8,128)}, f32[128,1792]{1,0:T(8,128)}, f32[1792,128]{1,0:T(8,128)}) custom-call(bf16[256,512]{1,0:T(8,128)(2,1)} %get-tuple-element.15.gx_in, f32[8,256]{1,0:T(8,128)} %get-tuple-element.16.dr_in, f32[128,1792]{1,0:T(8,128)} %get-tuple-element.17.dw0_in, ...), custom_call_target="tpu_custom_call" | custom-call | tf_op jit(solution)/shard_map/pallas_call | solution.py:744

commit v8 on v7

--- a/solution.py
+++ b/solution.py
@@ -501,6 +501,10 @@
         return (remote(dr_ref.at[1], dr_out, s_gx.at[0], r_gx.at[0], dev),
                 remote(gx_ref.at[1], gx_out, s_gx.at[1], r_gx.at[1], dev))
 
+    def own_sums():
+        return (pltpu.make_async_copy(gx_ref.at[0], gx_out, s_loc.at[3]),
+                pltpu.make_async_copy(dr_ref.at[0], dr_out, s_loc.at[4]))
+
     n_steps = len(END_STEPS)
 
     def stores(c):
@@ -584,6 +588,12 @@
                     dw2_ref[cols, :] = dwt_ref[:, cols].T
                     start_all(stores(c))
 
+                @pl.when(mid & (o == n_z - 1) & (c == CHUNKS - 2))
+                def _():
+                    with jax.named_scope("gather"):
+                        gather(0)
+                    start_all(own_sums())
+
                 return carry
 
             lo = pick([chosen(lambda t, n=n: t[1 + n][0], k) for n in range(n_z)], o)
@@ -596,12 +606,7 @@
 
     @pl.when(mid)
     def _():
-        with jax.named_scope("gather"):
-            gather(0)
-        own_sums = (pltpu.make_async_copy(gx_ref.at[0], gx_out, s_loc.at[3]),
-                    pltpu.make_async_copy(dr_ref.at[0], dr_out, s_loc.at[4]))
-        start_all(own_sums)
-        for c in own_sums:
+        for c in own_sums():
             c.wait()
         for way in (0, 1):
             @pl.when((z == 2) if way == 0 else (z == 1))

time: 146 us -> 146 us (level)
  no operation moved by 1% of the time
where the time goes in v8:
time: 146 us
  Pallas kernels  145 us (99%)
    pallas_call x1, Pallas kernels, per_device(): pl.pallas_call(functools.partial(kernel, cap, n_z, n_p), out_shape=(out((...  142 us
    pallas_call x1, Pallas kernels, per_device(): pl.pallas_call(finish, out_shape=(out((n_tok, d), BF16), out((top_k, n_to...  2.99 us

profile of v8, /device:TPU:0, one launch (start us, length us, event | category | flops | bytes accessed | tf_op | source)
XLA Modules:
  0.0 145.9 jit_solution(15286340363899935100)
XLA Ops:
  0.6 142.2 %shard_map.110 = (bf16[256,512]{1,0:T(8,128)(2,1)}, f32[8,256]{1,0:T(8,128)}, f32[128,1792]{1,0:T(8,128)}, f32[128,1792]{1,0:T(8,128)}, f32[1792,128]{1,0:T(8,128)}) custom-call(s32[2,256]{1,0:T(2,128)} %bitcast.6, f32[2,256]{1,0:T(2,128)} %bitcast.7, bf16[256,512]{1,0:T(8,128)(2,1)} %x_ref.1, bf16[256,512]{1,0:T(8,128)(2,1)} %dy_ref.1, ...), custom_call_target="tpu_custom_call" | custom-call | tf_op jit(solution)/shard_map/pallas_call | solution.py:707
  142.9 3.0 %shard_map.111 = (bf16[256,512]{1,0:T(8,128)(2,1)}, f32[2,256]{1,0:T(2,128)}, f32[128,1792]{1,0:T(8,128)}, f32[128,1792]{1,0:T(8,128)}, f32[1792,128]{1,0:T(8,128)}) custom-call(bf16[256,512]{1,0:T(8,128)(2,1)} %get-tuple-element.15.gx_in, f32[8,256]{1,0:T(8,128)} %get-tuple-element.16.dr_in, f32[128,1792]{1,0:T(8,128)} %get-tuple-element.17.dw0_in, ...), custom_call_target="tpu_custom_call" | custom-call | tf_op jit(solution)/shard_map/pallas_call | solution.py:749
